TPU v7x, 32 devices: a whole 2x2x4 slice. The times are simulated.
32 devices in a mesh: probe: 4 (over y, x), mp: 8 (over z, core).
Axes of the slice: x: 2, y: 2, z: 4, core: 2. Of those that a mesh axis runs over, the one named last changes fastest.
Arguments:
- tokens: bfloat16 [512, 2048], P('mp'), may hold values from -6 to 6
- targets: bfloat16 [512, 2048], P('mp'), may hold values from -6 to 6
- norm_gain: float32 [2048], replicated, may hold values from 0.5 to 1.5
- weights: bfloat16 [3, 5120, 2048], P(None, 'mp'), may hold values from -0.125 to 0.125
- probe_signs: bfloat16 [4, 3, 5120, 2048], P('probe', None, 'mp'), may hold values from -1 to 1, as said below
- m_state: float32 [3, 5120, 2048], P(None, 'mp'), may hold values from -0.3 to 0.3
- v_state: float32 [3, 2560, 16], P(None, 'mp'), may hold values from 0.0001 to 0.003
Outputs:
- hess_blocks: float32 [3, 2560, 16], P(None, 'mp')
- new_moment: float32 [3, 5120, 2048], P(None, 'mp')
- new_curvature: float32 [3, 2560, 16], P(None, 'mp')
- update: float32 [3, 5120, 2048], P(None, 'mp')
Inputs may be any that keep to these rules, and one draw needn't show every extreme that they name: `probe_signs`: every entry is +1 or -1, independently.
All inputs are finite; a program needn't handle non-finite values.
Results may differ from a plain program's by a relative error of at most 0.0026.
Values may be sent and summed in bfloat16 or wider, within the bound.
No kernel may reach another device: no remote copies, remote signals or barrier semaphores. Data moves between devices by JAX's collectives and lax.ppermute only.
A program may use at most 128 MiB of HBM per device.

v0:
```python
import functools

import jax
import jax.numpy as jnp
from jax import lax
from jax.experimental import pallas as pl
from jax.experimental.pallas import tpu as pltpu
from jax.sharding import PartitionSpec as P


BLOCK_ROWS = 2
BLOCK_COLS = 128
STEP = 4

beta_one = 0.9
beta_two = 0.999
epsilon = 0.0001
root_half = 0.7978845608028654
cubic = 0.044715

F32 = jnp.float32
BF16 = jnp.bfloat16


def gelu_parts(value):
    square = value * value
    inner = root_half * (value + cubic * square * value)
    slope_inner = root_half * (1.0 + 3.0 * cubic * square)
    curve_inner = 6.0 * root_half * cubic * value
    tangent = jnp.tanh(inner)
    damping = 1.0 - tangent * tangent
    activated = 0.5 * value * (1.0 + tangent)
    slope = 0.5 * (1.0 + tangent) + 0.5 * value * damping * slope_inner
    bend = damping * slope_inner + 0.5 * value * damping * (
        curve_inner - 2.0 * tangent * slope_inner * slope_inner
    )
    return (activated, slope, bend)


def dot_nt(left, right):
    return lax.dot_general(left, right, (((1,), (1,)), ((), ())), preferred_element_type=F32)


def dot_tn(left, right):
    return lax.dot_general(left, right, (((0,), (0,)), ((), ())), preferred_element_type=F32)


def dot_nn(left, right):
    return jnp.dot(left, right, preferred_element_type=F32)


FORWARD_UNITS = 320
TILT_UNITS = 320
SPREAD_COLS = 512
BASE_UNITS = 160
TANGENT_UNITS = 320
UPDATE_UNITS = 320
FORWARD_LIMIT = 48
BASE_LIMIT = 50
TANGENT_LIMIT = 50
UPDATE_LIMIT = 58


def unit_block(units, wanted):
    return wanted if units % wanted == 0 else units


def whole(shape):
    zeros = (0,) * len(shape)
    return pl.BlockSpec(shape, lambda *_: zeros, pipeline_mode=pl.Buffered(1))


def call(body, grid, in_specs, out_specs, out_shape, scratch, flops, traffic, limit, args):
    return pl.pallas_call(
        body,
        grid=grid,
        in_specs=in_specs,
        out_specs=out_specs,
        out_shape=out_shape,
        scratch_shapes=scratch,
        compiler_params=pltpu.CompilerParams(
            dimension_semantics=("arbitrary",) * len(grid), vmem_limit_bytes=limit * 1024 * 1024
        ),
        cost_estimate=pl.CostEstimate(flops=flops, bytes_accessed=traffic, transcendentals=0),
    )(*args)


def column_sums(values, kind, out):
    rows, width = values.shape
    lanes = lax.broadcasted_iota(jnp.int32, (rows, 128), 1)
    cols = width // BLOCK_COLS
    for at in range(cols):
        part = values[:, at * BLOCK_COLS : (at + 1) * BLOCK_COLS]
        out = jnp.where(lanes == kind * cols + at, jnp.sum(part, axis=1, keepdims=True), out)
    return out


def norm_kernel(tokens, gain, out):
    x = tokens[...].astype(F32)
    factor = lax.rsqrt(jnp.mean(x * x, axis=-1, keepdims=True) + 1e-06)
    out[...] = (x * factor * gain[...]).astype(BF16)


def norm(tokens, gain):
    rows, width = tokens.shape
    return call(
        norm_kernel,
        (1,),
        [whole((rows, width)), whole((1, width))],
        whole((rows, width)),
        jax.ShapeDtypeStruct((rows, width), BF16),
        [],
        rows * width * 4,
        rows * width * 4,
        8,
        (tokens, gain.reshape(1, width)),
    )


def joined(refs):
    return jnp.concatenate([ref[...] for ref in refs], axis=1)


def forward_kernel(pieces, refs):
    blocks = refs[:pieces]
    (w, x, p_out, g_out, s_out, b_out, hid_out, own_q, sib_q, acc_q) = refs[pieces:]
    step = pl.program_id(0)
    rows = blocks[0].shape[0]

    @pl.when(step == 0)
    def _():
        for at in range(pieces):
            x[at * rows : (at + 1) * rows] = blocks[at][...]

    units, width = w.shape[1:]
    pre = dot_nt(w[0:2].reshape(2 * units, width), x[...])
    pre_gate, pre_up = (pre[:units], pre[units:])
    activated, slope, bend = gelu_parts(pre_gate)
    p_out[...] = pre_up * slope
    g_out[...] = activated
    s_out[...] = slope
    b_out[...] = pre_up * bend
    hidden = (activated * pre_up).astype(BF16)
    hid_out[...] = hidden
    quarter = acc_q.shape[1]
    first = pl.multiple_of(lax.axis_index("probe") * quarter, quarter)
    add_q = dot_tn(hidden, w[2, :, pl.ds(first, quarter)])

    @pl.when(step == 0)
    def _():
        acc_q[...] = add_q

    @pl.when(step > 0)
    def _():
        acc_q[...] += add_q

    @pl.when(step == pl.num_programs(0) - 1)
    def _():
        half = own_q.shape[0]
        own_q[...] = acc_q[:half]
        sib_q[...] = acc_q[half:].astype(sib_q.dtype)


def forward(blocks, weights, quarter, sib_type):
    rows, width = blocks[0].shape
    count = rows * len(blocks)
    kinds, units, _ = weights.shape
    ub = unit_block(units, FORWARD_UNITS)
    half = count // 2
    unit_spec = pl.BlockSpec((ub, count), lambda i: (i, 0))
    shape = jax.ShapeDtypeStruct
    return call(
        lambda *refs: forward_kernel(len(blocks), refs),
        (units // ub,),
        [whole((rows, width))] * len(blocks)
        + [pl.BlockSpec((kinds, ub, width), lambda i: (0, i, 0))],
        [whole((count, width))] + [unit_spec] * 5 + [whole((half, quarter))] * 2,
        [shape((count, width), BF16)]
        + [shape((units, count), F32)] * 4
        + [
            shape((units, count), BF16),
            shape((half, quarter), F32),
            shape((half, quarter), sib_type),
        ],
        [pltpu.VMEM((count, quarter), F32)],
        2 * count * units * width * 2,
        units * width * 6 + units * count * 18 + count * width * 4,
        FORWARD_LIMIT,
        (*blocks, weights),
    )


def tilt_kernel(z, x, p, g, s, b, q_out, s_out, tan_out):
    units, width = z.shape[2:]
    tan = dot_nt(z[0].reshape(2 * units, width), x[...])
    tan_gate, tan_up = (tan[:units], tan[units:])
    slope = s[...]
    q_out[...] = tan_up * slope + b[...] * tan_gate
    s_out[...] = slope * tan_gate
    tan_out[...] = (p[...] * tan_gate + g[...] * tan_up).astype(BF16)


def tilt(signs, x, p, g, s, b):
    count, width = x.shape
    units = p.shape[0]
    ub = unit_block(units, TILT_UNITS)
    unit_spec = pl.BlockSpec((ub, count), lambda i: (i, 0))
    shape = jax.ShapeDtypeStruct
    return call(
        tilt_kernel,
        (units // ub,),
        [pl.BlockSpec((1, 2, ub, width), lambda i: (0, 0, i, 0)), whole((count, width))]
        + [unit_spec] * 4,
        [unit_spec] * 3,
        [shape((units, count), F32)] * 2 + [shape((units, count), BF16)],
        [],
        2 * count * units * width * 2,
        units * width * 4 + units * count * 26 + count * width * 2,
        FORWARD_LIMIT,
        (signs, x, p, g, s, b),
    )


def spread_kernel(parts, refs):
    (w, z) = refs[:2]
    tans = refs[2 : 2 + parts]
    hids = refs[2 + parts : 2 + 2 * parts]
    (own, sib, left) = refs[2 + 2 * parts :]
    units, count = hids[0].shape

    @pl.when(pl.program_id(0) == 0)
    def _():
        for at in range(parts):
            span = slice(at * count, (at + 1) * count)
            left[span, :units] = tans[at][...].T
            left[span, units:] = hids[at][...].T

    total = dot_nn(left[...], jnp.concatenate([w[0], z[0, 0]], axis=0))
    half = count // 2
    for at in range(parts):
        base_row = at * count
        own[at * half : (at + 1) * half] = total[base_row : base_row + half]
        sib[at * half : (at + 1) * half] = total[base_row + half : base_row + count].astype(
            sib.dtype
        )


def spread(weights, signs, tans, hids, sib_type):
    units, count = hids[0].shape
    parts = len(hids)
    width = weights.shape[2]
    half = parts * count // 2
    cols = SPREAD_COLS
    shape = jax.ShapeDtypeStruct
    out_spec = pl.BlockSpec((half, cols), lambda i: (0, i))
    return call(
        lambda *refs: spread_kernel(parts, refs),
        (width // cols,),
        [
            pl.BlockSpec((1, units, cols), lambda i: (2, 0, i)),
            pl.BlockSpec((1, 1, units, cols), lambda i: (0, 2, 0, i)),
        ]
        + [whole((units, count))] * (2 * parts),
        [out_spec, out_spec],
        [shape((half, width), F32), shape((half, width), sib_type)],
        [pltpu.VMEM((parts * count, 2 * units), BF16)],
        4 * parts * count * units * width,
        units * width * 4 + half * width * 6,
        FORWARD_LIMIT,
        (weights, signs, *tans, *hids),
    )


def base_kernel(pieces, parts, refs):
    blocks = refs[: 2 * pieces]
    refs = refs[2 * pieces :]
    (w, z, m) = refs[:3]
    groups = [refs[3 + at * parts : 3 + (at + 1) * parts] for at in range(7)]
    (xs, ps, gs, qs, ss, hids, tans) = groups
    (new_m, e_gate, e_up, sums, normed, dout) = refs[3 + 7 * parts :]
    step = pl.program_id(0)
    half, quarter = blocks[0].shape
    chunk = 2 * half // parts

    @pl.when(step == 0)
    def _():
        me = lax.axis_index("probe")
        for at in range(pieces):
            first = pl.multiple_of((me ^ at) * quarter, quarter)
            for side in range(2):
                source = blocks[side * pieces + at]
                for part in range(parts):
                    start = part * chunk + side * (chunk // 2)
                    dout[start : start + chunk // 2, pl.ds(first, quarter)] = source[
                        part * (chunk // 2) : (part + 1) * (chunk // 2)
                    ]
        for part in range(parts):
            normed[part * chunk : (part + 1) * chunk] = xs[part][...]

    units = m.shape[1]
    d = dout[...]
    both = dot_nt(jnp.concatenate([w[0], z[0, 0]], axis=0), d)
    dhid, sdhid = (both[:units], both[units:])
    pv, gv = (joined(ps), joined(gs))
    e_gate[...] = sdhid * pv + dhid * joined(qs)
    e_up[...] = sdhid * gv + dhid * joined(ss)
    inner = jnp.concatenate([(dhid * pv).astype(BF16), (dhid * gv).astype(BF16)], axis=0)
    grads = dot_nn(inner, normed[...])
    new_m[0] = beta_one * m[0] + (1.0 - beta_one) * grads[:units]
    new_m[1] = beta_one * m[1] + (1.0 - beta_one) * grads[units:]
    outer = dot_nn(jnp.concatenate([joined(hids), joined(tans)], axis=0), d)
    new_m[2] = beta_one * m[2] + (1.0 - beta_one) * outer[:units]
    sums[...] = column_sums(z[0, 0].astype(F32) * outer[units:], 2, jnp.zeros((units, 128), F32))


def base(pieces, weights, signs, m, xs, ps, gs, qs, ss, hids, tans):
    half, quarter = pieces[0].shape
    kinds, units, width = weights.shape
    count = 2 * half
    parts = len(xs)
    chunk = count // parts
    ub = unit_block(units, BASE_UNITS)
    unit_spec = pl.BlockSpec((ub, count), lambda i: (i, 0))
    chunk_spec = pl.BlockSpec((ub, chunk), lambda i: (i, 0))
    mat_spec = pl.BlockSpec((kinds, ub, width), lambda i: (0, i, 0))
    sum_spec = pl.BlockSpec((ub, 128), lambda i: (i, 0))
    shape = jax.ShapeDtypeStruct
    return call(
        lambda *refs: base_kernel(len(pieces) // 2, parts, refs),
        (units // ub,),
        [whole((half, quarter))] * len(pieces)
        + [
            pl.BlockSpec((1, ub, width), lambda i: (2, i, 0)),
            pl.BlockSpec((1, 1, ub, width), lambda i: (0, 2, i, 0)),
            mat_spec,
        ]
        + [whole((chunk, width))] * parts
        + [chunk_spec] * (6 * parts),
        [mat_spec, unit_spec, unit_spec, sum_spec, whole((count, width))],
        [
            shape((kinds, units, width), F32),
            shape((units, count), F32),
            shape((units, count), F32),
            shape((units, 128), F32),
            shape((count, width), BF16),
        ],
        [pltpu.VMEM((count, width), BF16)],
        2 * count * units * width * 6,
        units * width * 28 + units * count * 28,
        BASE_LIMIT,
        (*pieces, weights, signs, m, *xs, *ps, *gs, *qs, *ss, *hids, *tans),
    )


def tangent_kernel(pieces, parts, refs):
    blocks = refs[:pieces]
    (w, z, normed, e_gate, e_up, sums_in) = refs[pieces : pieces + 6]
    refs = refs[pieces + 6 :]
    (ps, gs, hids) = [refs[at * parts : (at + 1) * parts] for at in range(3)]
    (sums, tdout, rows_sum, pairs) = refs[3 * parts :]
    step = pl.program_id(0)
    rows = blocks[0].shape[0]

    @pl.when(step == 0)
    def _():
        for at in range(pieces):
            tdout[at * rows : (at + 1) * rows] = blocks[at][...]

    units = e_gate.shape[0]
    t = tdout[...]
    tdh = dot_nt(w[0], t)
    inner = jnp.concatenate(
        [
            (tdh * joined(ps) + e_gate[...]).astype(BF16),
            (tdh * joined(gs) + e_up[...]).astype(BF16),
        ],
        axis=0,
    )
    hv = dot_nn(inner, normed[...])
    hv_out = dot_nn(joined(hids), t)
    made = jnp.zeros((units, 128), F32)
    made = column_sums(z[0, 0].astype(F32) * hv[:units], 0, made)
    made = column_sums(z[0, 1].astype(F32) * hv[units:], 1, made)
    made = column_sums(z[0, 2].astype(F32) * hv_out, 2, made)
    rows_sum[...] = made + sums_in[...]
    half = units // BLOCK_ROWS
    pairs[pl.ds(pl.multiple_of(step * half, 8), half), :] = (
        rows_sum[pl.ds(0, half, stride=2), :] + rows_sum[pl.ds(1, half, stride=2), :]
    )

    @pl.when(step == pl.num_programs(0) - 1)
    def _():
        sums[...] = pairs[...].T[: sums.shape[0]]


def tangent(blocks, weights, signs, normed, e_gate, e_up, sums, ps, gs, hids):
    rows, width = blocks[0].shape
    count = normed.shape[0]
    kinds, units, _ = weights.shape
    parts = len(ps)
    ub = unit_block(units, TANGENT_UNITS)
    unit_spec = pl.BlockSpec((ub, count), lambda i: (i, 0))
    chunk_spec = pl.BlockSpec((ub, count // parts), lambda i: (i, 0))
    cols = width // BLOCK_COLS
    return call(
        lambda *refs: tangent_kernel(len(blocks), parts, refs),
        (units // ub,),
        [whole((rows, width))] * len(blocks)
        + [
            pl.BlockSpec((1, ub, width), lambda i: (2, i, 0)),
            pl.BlockSpec((1, kinds, ub, width), lambda i: (0, 0, i, 0)),
            whole((count, width)),
            unit_spec,
            unit_spec,
            pl.BlockSpec((ub, 128), lambda i: (i, 0)),
        ]
        + [chunk_spec] * (3 * parts),
        whole((kinds * cols, units // BLOCK_ROWS)),
        jax.ShapeDtypeStruct((kinds * cols, units // BLOCK_ROWS), F32),
        [
            pltpu.VMEM((count, width), BF16),
            pltpu.VMEM((ub, 128), F32),
            pltpu.VMEM((units // BLOCK_ROWS, 128), F32),
        ],
        2 * count * units * width * 4,
        units * width * 8 + units * count * 18,
        TANGENT_LIMIT,
        (*blocks, weights, signs, normed, e_gate, e_up, sums, *ps, *gs, *hids),
    )


def update_kernel(probes, a, b, c, d, v, m, hess, new_v, update, scales):
    kinds, cols, half = v.shape
    kind, step = (pl.program_id(0), pl.program_id(1))

    @pl.when((kind == 0) & (step == 0))
    def _():
        total = (a[...] + b[...]) + (c[...] + d[...])
        for at in range(kinds):
            h = total[at * cols : (at + 1) * cols] * (1.0 / (BLOCK_ROWS * BLOCK_COLS * probes))
            hess[at] = h
            nv = beta_two * v[at] + (1.0 - beta_two) * h * h
            new_v[at] = nv
            denom = jnp.sqrt(nv / (1.0 - beta_two**STEP)) + epsilon
            scale = 1.0 / (denom * (1.0 - beta_one**STEP))
            wide = jnp.concatenate([scale, jnp.zeros((128 - cols, half), F32)], axis=0).T
            scales[at, pl.ds(0, half, stride=2), :] = wide
            scales[at, pl.ds(1, half, stride=2), :] = wide

    tall = m.shape[1]
    full = scales[kind, pl.ds(pl.multiple_of(step * tall, tall), tall), :]
    for at in range(cols):
        span = slice(at * BLOCK_COLS, (at + 1) * BLOCK_COLS)
        update[0, :, span] = m[0, :, span] * full[:, at : at + 1]


def update_step(sums, v, m):
    kinds, units, width = m.shape
    ub = unit_block(units, UPDATE_UNITS)
    m_spec = pl.BlockSpec((1, ub, width), lambda k, i: (k, i, 0))
    shape = jax.ShapeDtypeStruct
    return call(
        functools.partial(update_kernel, len(sums)),
        (kinds, units // ub),
        [whole(sums[0].shape)] * 4 + [whole(v.shape), m_spec],
        [whole(v.shape), whole(v.shape), m_spec],
        [shape(v.shape, F32), shape(v.shape, F32), shape(m.shape, F32)],
        [pltpu.VMEM((kinds, units, 128), F32)],
        units * width * 6,
        units * width * 24,
        UPDATE_LIMIT,
        (*sums, v, m),
    )


def to_sibling(x, chips):
    return lax.ppermute(x, "mp", [(i, i ^ 1) for i in range(2 * chips)])


def to_chip(x, chips, flip):
    pairs = [(2 * z + c, 2 * (z ^ flip) + c) for z in range(chips) for c in range(2)]
    return lax.ppermute(x, "mp", pairs)


def to_probe(x, probes, flip):
    return lax.ppermute(x, "probe", [(i, i ^ flip) for i in range(probes)])


def gather_rows(x, chips):
    own = [x]
    for flip in range(1, chips):
        own.append(to_chip(x, chips, flip))
    sib = []
    for flip in range(chips):
        sib.append(to_sibling(own[flip], chips))
    half = chips // 2
    return [own[:half] + sib[:half], own[half:] + sib[half:]]


def near_path(normed, offset, weights, probe_signs, m_state, chips, probes):
    rows, width = normed.shape
    count = 2 * chips * rows
    quarter = width // probes
    chunks = gather_rows(normed, chips)
    xs, ps, gs, qs, ss, hids, tans, totals = ([], [], [], [], [], [], [], [])
    for blocks in chunks:
        x, p, g, s, b, hid, own_q, sib_q = forward(blocks, weights, quarter, BF16)
        got = to_sibling(sib_q, chips)
        totals.append(own_q + got.astype(F32))
        q, s, tan = tilt(probe_signs, x, p, g, s, b)
        for held, value in zip((xs, ps, gs, qs, ss, hids, tans), (x, p, g, q, s, hid, tan)):
            held.append(value)
    own_t, sib_t = spread(weights, probe_signs, tans, hids, BF16)
    kept = totals[0][:rows] + offset
    for flip in range(1, chips):
        part = totals[flip // 2][(flip % 2) * rows : (flip % 2 + 1) * rows].astype(BF16)
        kept = kept + to_chip(part, chips, flip).astype(F32)
    part = (kept / count).astype(BF16)
    mine = [part]
    for flip in range(1, chips):
        mine.append(to_chip(part, chips, flip))
    mine = jnp.concatenate(mine, axis=0)
    pieces = [mine]
    for flip in range(1, probes):
        pieces.append(to_probe(mine, probes, flip))
    for at in range(probes):
        pieces.append(to_sibling(pieces[at], chips))
    got = to_sibling(sib_t, chips)
    total = own_t + got.astype(F32)
    kept = total[:rows]
    for flip in range(1, chips):
        part = total[flip * rows : (flip + 1) * rows].astype(BF16)
        kept = kept + to_chip(part, chips, flip).astype(F32)
    tan_dout = (kept / count).astype(BF16)
    tan_blocks = gather_rows(tan_dout, chips)
    new_m, e_gate, e_up, sums, full = base(
        pieces, weights, probe_signs, m_state, xs, ps, gs, qs, ss, hids, tans
    )
    sums = tangent(
        tan_blocks[0] + tan_blocks[1],
        weights,
        probe_signs,
        full,
        e_gate,
        e_up,
        sums,
        ps,
        gs,
        hids,
    )
    return new_m, sums


def far_path(normed, offset, weights, probe_signs, m_state, chips, probes):
    rows, width = normed.shape
    count = 2 * chips * rows
    quarter = width // probes
    blocks = [lax.all_gather(normed, "mp", axis=0, tiled=True)]
    x, p, g, s, b, hid, own_q, sib_q = forward(blocks, weights, quarter, F32)
    q, s, tan = tilt(probe_signs, x, p, g, s, b)
    own_t, sib_t = spread(weights, probe_signs, [tan], [hid], F32)
    part = lax.psum_scatter(
        jnp.concatenate([own_q, sib_q], axis=0), "mp", scatter_dimension=0, tiled=True
    )
    mine = lax.all_gather(
        ((part + offset) / count).astype(BF16), "mp", axis=0, tiled=True
    )
    pieces = [mine] + [to_probe(mine, probes, flip) for flip in range(1, probes)]
    half = count // 2
    pieces = [piece[:half] for piece in pieces] + [piece[half:] for piece in pieces]
    kept = lax.psum_scatter(
        jnp.concatenate([own_t, sib_t], axis=0), "mp", scatter_dimension=0, tiled=True
    )
    tan_blocks = [lax.all_gather((kept / count).astype(BF16), "mp", axis=0, tiled=True)]
    new_m, e_gate, e_up, sums, full = base(
        pieces, weights, probe_signs, m_state, [x], [p], [g], [q], [s], [hid], [tan]
    )
    sums = tangent(
        tan_blocks, weights, probe_signs, full, e_gate, e_up, sums, [p], [g], [hid]
    )
    return new_m, sums


def shards(tokens, targets, norm_gain, weights, probe_signs, m_state, v_state):
    probes = lax.axis_size("probe")
    chips = lax.axis_size("mp") // 2
    quarter = tokens.shape[1] // probes
    first = lax.axis_index("probe") * quarter
    normed = norm(tokens, norm_gain)
    offset = lax.dynamic_slice_in_dim(tokens, first, quarter, 1).astype(
        F32
    ) - lax.dynamic_slice_in_dim(targets, first, quarter, 1).astype(F32)
    path = near_path if chips == 4 else far_path
    new_m, sums = path(normed, offset, weights, probe_signs, m_state, chips, probes)
    sums = [sums] + [to_probe(sums, probes, flip) for flip in range(1, probes)]
    hess, new_v, update = update_step(sums, v_state.transpose(0, 2, 1), new_m)
    return (hess.transpose(0, 2, 1), new_m, new_v.transpose(0, 2, 1), update)


def solution(mesh):
    return jax.shard_map(
        shards,
        mesh=mesh,
        in_specs=(
            P("mp", None),
            P("mp", None),
            P(),
            P(None, "mp", None),
            P("probe", None, "mp", None),
            P(None, "mp", None),
            P(None, "mp", None),
        ),
        out_specs=(
            P(None, "mp", None),
            P(None, "mp", None),
            P(None, "mp", None),
            P(None, "mp", None),
        ),
        check_vma=False,
    )
```

profile of v0, /device:TPU:0, one launch (start us, length us, event | category | flops | bytes accessed | tf_op | source)
XLA Modules:
  0.0 181.6 jit_solution(17259051042591627453)
XLA Ops:
  2.4 4.1 %collective-permute-start.3 = (bf16[64,2048]{1,0:T(8,128)(2,1)S(1)}, bf16[64,2048]{1,0:T(8,128)(2,1)S(1)}, u32[]{:S(2)}, u32[]{:S(2)}) collective-permute-start(bf16[64,2048]{1,0:T(8,128)(2,1)S(1)} %shard_map.102.refs_0_), channel_id=1, source_target_pairs={{0,4},{1,5},{2,6},{3,7},{4,0},{5,1},{6,2},{7,3},{8,12},{9,13},{10,... | collective-permute-start | bytes 786440 | tf_op jit(solution)/shard_map/ppermute | solution.py:482
  6.6 1.3 collective-permute-start.4
  8.2 16.9 %collective-permute-done.3.refs_0_ = bf16[64,2048]{1,0:T(8,128)(2,1)S(1)} collective-permute-done((bf16[64,2048]{1,0:T(8,128)(2,1)S(1)}, bf16[64,2048]{1,0:T(8,128)(2,1)S(1)}, u32[]{:S(2)}, u32[]{:S(2)}) %collective-permute-start.3) | collective-permute-done | bytes 262176 | tf_op jit(solution)/shard_map/ppermute | solution.py:482
  26.9 5.6 %shard_map.105 = (bf16[256,2048]{1,0:T(8,128)(2,1)S(1)}, f32[640,256]{1,0:T(8,128)S(1)}, f32[640,256]{1,0:T(8,128)S(1)}, f32[640,256]{1,0:T(8,128)S(1)}, f32[640...) custom-call(bf16[64,2048]{1,0:T(8,128)(2,1)S(1)} %collective-permute-done, ...), custom_call_target="tpu_custom_call" | custom-call | flops 1342177280 | bytes 12910592 | tf_op jit(solution)/shard_map/pallas_call | solution.py:74
  32.8 6.2 %shard_map.103 = (bf16[256,2048]{1,0:T(8,128)(2,1)S(1)}, f32[640,256]{1,0:T(8,128)S(1)}, f32[640,256]{1,0:T(8,128)S(1)}, f32[640,256]{1,0:T(8,128)S(1)}, f32[640...) custom-call(bf16[64,2048]{1,0:T(8,128)(2,1)S(1)} %shard_map.102.refs_0_, ...), custom_call_target="tpu_custom_call" | custom-call | flops 1342177280 | bytes 12910592 | tf_op jit(solution)/shard_map/pallas_call | solution.py:74
  39.3 4.2 %shard_map.106 = (f32[640,256]{1,0:T(8,128)S(1)}, f32[640,256]{1,0:T(8,128)S(1)}, bf16[640,256]{1,0:T(8,128)(2,1)S(1)}) custom-call(bf16[1,3,640,2048]{3,2,1,0:T(8,128)(2,1)} %refs_9_.3, bf16[256,2048]{1,0:T(8,128)(2,1)S(1)} %get-tuple-element.42.x.refs_12_, f32[640,256]{1,0:T(8,128)S(1)} %get-tuple-element.43.p.refs_14_.refs_15_, ...), custom_call_target="tpu_custom_call" | custom-call | flops 1342177280 | bytes 10551296 | tf_op jit(solution)/shard_map/pallas_call | solution.py:74
  45.2 3.7 %shard_map.104 = (f32[640,256]{1,0:T(8,128)S(1)}, f32[640,256]{1,0:T(8,128)S(1)}, bf16[640,256]{1,0:T(8,128)(2,1)S(1)}) custom-call(bf16[1,3,640,2048]{3,2,1,0:T(8,128)(2,1)} %refs_9_.3, bf16[256,2048]{1,0:T(8,128)(2,1)S(1)} %get-tuple-element.36.x.refs_11_, f32[640,256]{1,0:T(8,128)S(1)} %get-tuple-element.37.p.refs_13_.refs_14_, ...), custom_call_target="tpu_custom_call" | custom-call | flops 1342177280 | bytes 10551296 | tf_op jit(solution)/shard_map/pallas_call | solution.py:74
  48.9 7.1 %shard_map.107 = (f32[256,2048]{1,0:T(8,128)S(1)}, bf16[256,2048]{1,0:T(8,128)(2,1)}) custom-call(bf16[3,640,2048]{2,1,0:T(8,128)(2,1)} %refs_8_.3, bf16[1,3,640,2048]{3,2,1,0:T(8,128)(2,1)} %refs_9_.3, bf16[640,256]{1,0:T(8,128)(2,1)S(1)} %get-tuple-element.41.refs_2_.refs_23_, bf16[640,256]{1,0:T(8,128)(2,1)S(1)} %get-tuple-element.47.refs_3_.refs_24_, ...), custom_call_target="tpu_custom_call" | custom-call | flops 2684354560 | bytes 8388608 | tf_op jit(solution)/shard_map/pallas_call | solution.py:74
  56.2 7.1 %collective-permute-start.21 = (bf16[64,512]{1,0:T(8,128)(2,1)S(1)}, bf16[64,512]{1,0:T(8,128)(2,1)S(1)}, u32[]{:S(2)}, u32[]{:S(2)}) collective-permute-start(bf16[64,512]{1,0:T(8,128)(2,1)S(1)} %get-tuple-element.73), channel_id=1, source_target_pairs={{0,4},{1,5},{2,6},{3,7},{4,0},{5,1},{6,2},{7,3},{8,12},{9,13},{10,... | collective-permute-start | bytes 196616 | tf_op jit(solution)/shard_map/ppermute | solution.py:482
  64.1 3.6 %collective-permute-done.21 = bf16[64,512]{1,0:T(8,128)(2,1)S(1)} collective-permute-done((bf16[64,512]{1,0:T(8,128)(2,1)S(1)}, bf16[64,512]{1,0:T(8,128)(2,1)S(1)}, u32[]{:S(2)}, u32[]{:S(2)}) %collective-permute-start.21) | collective-permute-done | bytes 65568 | tf_op jit(solution)/shard_map/ppermute | solution.py:482
  67.6 2.3 %collective-permute-done.22 = bf16[64,512]{1,0:T(8,128)(2,1)S(1)} collective-permute-done((bf16[64,512]{1,0:T(8,128)(2,1)S(1)}, bf16[64,512]{1,0:T(8,128)(2,1)S(1)}, u32[]{:S(2)}, u32[]{:S(2)}) %collective-permute-start.22) | collective-permute-done | bytes 65568 | tf_op jit(solution)/shard_map/ppermute | solution.py:482
  71.7 2.0 %collective-permute-start.24 = (bf16[64,512]{1,0:T(8,128)(2,1)S(1)}, bf16[64,512]{1,0:T(8,128)(2,1)S(1)}, u32[]{:S(2)}, u32[]{:S(2)}) collective-permute-start(bf16[64,512]{1,0:T(8,128)(2,1)S(1)} %fusion.8), channel_id=1, source_target_pairs={{0,4},{1,5},{2,6},{3,7},{4,0},{5,1},{6,2},{7,3},{8,12},{9,13},{10,... | collective-permute-start | bytes 196616 | tf_op jit(solution)/shard_map/ppermute | solution.py:482
  73.7 1.8 %collective-permute-start.25 = (bf16[64,512]{1,0:T(8,128)(2,1)S(1)}, bf16[64,512]{1,0:T(8,128)(2,1)S(1)}, u32[]{:S(2)}, u32[]{:S(2)}) collective-permute-start(bf16[64,512]{1,0:T(8,128)(2,1)S(1)} %fusion.8), channel_id=1, source_target_pairs={{0,6},{1,7},{2,4},{3,5},{4,2},{5,3},{6,0},{7,1},{8,14},{9,15},{10,... | collective-permute-start | bytes 196616 | tf_op jit(solution)/shard_map/ppermute | solution.py:482
  76.1 2.8 %collective-permute-done.24 = bf16[64,512]{1,0:T(8,128)(2,1)S(1)} collective-permute-done((bf16[64,512]{1,0:T(8,128)(2,1)S(1)}, bf16[64,512]{1,0:T(8,128)(2,1)S(1)}, u32[]{:S(2)}, u32[]{:S(2)}) %collective-permute-start.24) | collective-permute-done | bytes 65568 | tf_op jit(solution)/shard_map/ppermute | solution.py:482
  79.9 1.6 collective-permute-start.26
  81.5 1.5 collective-permute-start.27
  83.0 1.6 fusion.9
  84.7 1.8 collective-permute-start.10
  86.8 2.4 %collective-permute-start.9 = (bf16[64,2048]{1,0:T(8,128)(2,1)S(1)}, bf16[64,2048]{1,0:T(8,128)(2,1)S(1)}, u32[]{:S(2)}, u32[]{:S(2)}) collective-permute-start(bf16[64,2048]{1,0:T(8,128)(2,1)S(1)} %get-tuple-element.72), channel_id=1, source_target_pairs={{0,4},{1,5},{2,6},{3,7},{4,0},{5,1},{6,2},{7,3},{8,12},{9,13},{10,... | collective-permute-start | bytes 786440 | tf_op jit(solution)/shard_map/ppermute | solution.py:482
  89.6 6.1 %collective-permute-done.10 = bf16[64,2048]{1,0:T(8,128)(2,1)S(1)} collective-permute-done((bf16[64,2048]{1,0:T(8,128)(2,1)S(1)}, bf16[64,2048]{1,0:T(8,128)(2,1)S(1)}, u32[]{:S(2)}, u32[]{:S(2)}) %collective-permute-start.10) | collective-permute-done | bytes 262176 | tf_op jit(solution)/shard_map/ppermute | solution.py:482
  95.7 5.3 %collective-permute-done.8 = bf16[64,2048]{1,0:T(8,128)(2,1)S(1)} collective-permute-done((bf16[64,2048]{1,0:T(8,128)(2,1)S(1)}, bf16[64,2048]{1,0:T(8,128)(2,1)S(1)}, u32[]{:S(2)}, u32[]{:S(2)}) %collective-permute-start.8) | collective-permute-done | bytes 262176 | tf_op jit(solution)/shard_map/ppermute | solution.py:482
  101.1 12.4 %collective-permute-done.9 = bf16[64,2048]{1,0:T(8,128)(2,1)S(1)} collective-permute-done((bf16[64,2048]{1,0:T(8,128)(2,1)S(1)}, bf16[64,2048]{1,0:T(8,128)(2,1)S(1)}, u32[]{:S(2)}, u32[]{:S(2)}) %collective-permute-start.9) | collective-permute-done | bytes 262176 | tf_op jit(solution)/shard_map/ppermute | solution.py:482
  113.7 2.9 %collective-permute-start.14 = (bf16[64,2048]{1,0:T(8,128)(2,1)S(1)}, bf16[64,2048]{1,0:T(8,128)(2,1)S(1)}, u32[]{:S(2)}, u32[]{:S(2)}) collective-permute-start(bf16[64,2048]{1,0:T(8,128)(2,1)S(1)} %fusion.3.refs_0_), channel_id=1, source_target_pairs={{0,4},{1,5},{2,6},{3,7},{4,0},{5,1},{6,2},{7,3},{8,12},{9,13},{10,... | collective-permute-start | bytes 786440 | tf_op jit(solution)/shard_map/ppermute | solution.py:482
  116.6 1.5 collective-permute-start.15
  118.6 3.6 %collective-permute-done.11.refs_1_ = bf16[64,2048]{1,0:T(8,128)(2,1)S(1)} collective-permute-done((bf16[64,2048]{1,0:T(8,128)(2,1)S(1)}, bf16[64,2048]{1,0:T(8,128)(2,1)S(1)}, u32[]{:S(2)}, u32[]{:S(2)}) %collective-permute-start.11) | collective-permute-done | bytes 262176 | tf_op jit(solution)/shard_map/ppermute | solution.py:482
  122.2 4.5 %collective-permute-done.14.refs_4_ = bf16[64,2048]{1,0:T(8,128)(2,1)S(1)} collective-permute-done((bf16[64,2048]{1,0:T(8,128)(2,1)S(1)}, bf16[64,2048]{1,0:T(8,128)(2,1)S(1)}, u32[]{:S(2)}, u32[]{:S(2)}) %collective-permute-start.14) | collective-permute-done | bytes 262176 | tf_op jit(solution)/shard_map/ppermute | solution.py:482
  127.2 20.8 %shard_map.108 = (f32[3,640,2048]{2,1,0:T(8,128)}, f32[640,512]{1,0:T(8,128)}, f32[640,512]{1,0:T(8,128)}, f32[640,128]{1,0:T(8,128)S(1)}, bf16[512,2048]{1,0:T(8,128)(2,1)}) custom-call(bf16[256,512]{1,0:T(8,128)(2,1)S(1)} %pad_maximum_fusion.refs_0_, bf16[256,512]{1,0:T(8,128)(2,1)S(1)} %collective-permute-done.26.refs_1_, ...), custom_call_target="tpu_custom_call" | custom-call | flops 8053063680 | bytes 45875200 | tf_op jit(solution)/shard_map/pallas_call | solution.py:74
  148.1 10.9 %shard_map.109.a = f32[48,320]{1,0:T(8,128)S(1)} custom-call(bf16[64,2048]{1,0:T(8,128)(2,1)S(1)} %fusion.3.refs_0_, bf16[64,2048]{1,0:T(8,128)(2,1)S(1)} %collective-permute-done.11.refs_1_, bf16[64,2048]{1,0:T(8,128)(2,1)S(1)} %collective-permute-done.12.refs_2_, bf16[64,2048]{1,0:T(8,128)(2,1)S(1)} %collective-permute-done.13.refs_3_, ...), custom_call_target="tpu_custom_call" | custom-call | flops 5368709120 | bytes 16384000 | tf_op jit(solution)/shard_map/pallas_call | solution.py:74
  159.6 2.1 %collective-permute-start.34 = (f32[48,320]{1,0:T(8,128)S(1)}, f32[48,320]{1,0:T(8,128)S(1)}, u32[]{:S(2)}, u32[]{:S(2)}) collective-permute-start(f32[48,320]{1,0:T(8,128)S(1)} %shard_map.109.a), channel_id=1, source_target_pairs={{0,16},{8,24},{16,0},{24,8},{1,17},{9,25},{17,1},{25,9},{2,18},{10... | collective-permute-start | bytes 184328 | tf_op jit(solution)/shard_map/ppermute | solution.py:486
  163.5 1.7 collective-permute-done.34.c
  165.2 1.8 collective-permute-done.35.d
  167.6 14.0 %shard_map.110 = (f32[3,16,320]{2,1,0:T(8,128)}, f32[3,16,320]{2,1,0:T(8,128)}, f32[3,640,2048]{2,1,0:T(8,128)}) custom-call(f32[48,320]{1,0:T(8,128)} %copy-done.16, f32[48,320]{1,0:T(8,128)} %copy-done.18, f32[48,320]{1,0:T(8,128)} %copy-done.19, f32[48,320]{1,0:T(8,128)} %copy-done.20, f32[3,16,320]{2,1,0:T(8,128)} %bitcast.5, ...), custom_call_target="tpu_custom_call" | custom-call | flops 7864320 | bytes 31457280 | tf_op jit(solution)/shard_map/pallas_call | solution.py:74
  (100 shorter events, 15.6 us)
Async XLA Ops:
  2.4 22.6 %collective-permute-start.3 = (bf16[64,2048]{1,0:T(8,128)(2,1)S(1)}, bf16[64,2048]{1,0:T(8,128)(2,1)S(1)}, u32[]{:S(2)}, u32[]{:S(2)}) collective-permute-start(bf16[64,2048]{1,0:T(8,128)(2,1)S(1)} %shard_map.102.refs_0_), channel_id=1, source_target_pairs={{0,4},{1,5},{2,6},{3,7},{4,0},{5,1},{6,2},{7,3},{8,12},{9,13},{10,... | collective-permute-start | bytes 786440 | tf_op jit(solution)/shard_map/ppermute | solution.py:482
  6.6 18.4 %collective-permute-start.4 = (bf16[64,2048]{1,0:T(8,128)(2,1)S(1)}, bf16[64,2048]{1,0:T(8,128)(2,1)S(1)}, u32[]{:S(2)}, u32[]{:S(2)}) collective-permute-start(bf16[64,2048]{1,0:T(8,128)(2,1)S(1)} %shard_map.102.refs_0_), channel_id=1, source_target_pairs={{0,6},{1,7},{2,4},{3,5},{4,2},{5,3},{6,0},{7,1},{8,14},{9,15},{10,... | collective-permute-start | bytes 786440 | tf_op jit(solution)/shard_map/ppermute | solution.py:482
  7.9 17.6 %collective-permute-start = (bf16[64,2048]{1,0:T(8,128)(2,1)S(1)}, bf16[64,2048]{1,0:T(8,128)(2,1)S(1)}, u32[]{:S(2)}, u32[]{:S(2)}) collective-permute-start(bf16[64,2048]{1,0:T(8,128)(2,1)S(1)} %shard_map.102.refs_0_), channel_id=1, source_target_pairs={{0,2},{1,3},{2,0},{3,1},{4,6},{5,7},{6,4},{7,5},{8,10},{9,11},{10,... | collective-permute-start | bytes 786440 | tf_op jit(solution)/shard_map/ppermute | solution.py:482
  25.5 7.3 %collective-permute-start.1 = (bf16[64,2048]{1,0:T(8,128)(2,1)S(1)}, bf16[64,2048]{1,0:T(8,128)(2,1)S(1)}, u32[]{:S(2)}, u32[]{:S(2)}) collective-permute-start(bf16[64,2048]{1,0:T(8,128)(2,1)S(1)} %shard_map.102.refs_0_), channel_id=1, source_target_pairs={{0,1},{1,0},{2,3},{3,2},{4,5},{5,4},{6,7},{7,6},{8,9},{9,8},{10,11... | collective-permute-start | bytes 786440 | tf_op jit(solution)/shard_map/ppermute | solution.py:477
  25.5 7.3 %collective-permute-start.2 = (bf16[64,2048]{1,0:T(8,128)(2,1)S(1)}, bf16[64,2048]{1,0:T(8,128)(2,1)S(1)}, u32[]{:S(2)}, u32[]{:S(2)}) collective-permute-start(bf16[64,2048]{1,0:T(8,128)(2,1)S(1)} %collective-permute-done.refs_1_), channel_id=1, source_target_pairs={{0,1},{1,0},{2,3},{3,2},{4,5},{5,4},{6,7},{7,6},{8,9},{9,8},{10,11... | collective-permute-start | bytes 786440 | tf_op jit(solution)/shard_map/ppermute | solution.py:477
  32.6 23.6 %collective-permute-start.20 = (bf16[128,512]{1,0:T(8,128)(2,1)S(1)}, bf16[128,512]{1,0:T(8,128)(2,1)S(1)}, u32[]{:S(2)}, u32[]{:S(2)}) collective-permute-start(bf16[128,512]{1,0:T(8,128)(2,1)S(1)} %get-tuple-element.55), channel_id=1, source_target_pairs={{0,1},{1,0},{2,3},{3,2},{4,5},{5,4},{6,7},{7,6},{8,9},{9,8},{10,11... | collective-permute-start | bytes 393224 | tf_op jit(solution)/shard_map/ppermute | solution.py:477
  39.0 24.7 %collective-permute-start.18 = (bf16[128,512]{1,0:T(8,128)(2,1)S(1)}, bf16[128,512]{1,0:T(8,128)(2,1)S(1)}, u32[]{:S(2)}, u32[]{:S(2)}) collective-permute-start(bf16[128,512]{1,0:T(8,128)(2,1)S(1)} %get-tuple-element.53), channel_id=1, source_target_pairs={{0,1},{1,0},{2,3},{3,2},{4,5},{5,4},{6,7},{7,6},{8,9},{9,8},{10,11... | collective-permute-start | bytes 393224 | tf_op jit(solution)/shard_map/ppermute | solution.py:477
  56.0 27.0 %collective-permute-start.7 = (bf16[256,2048]{1,0:T(8,128)(2,1)}, bf16[256,2048]{1,0:T(8,128)(2,1)}, u32[]{:S(2)}, u32[]{:S(2)}) collective-permute-start(bf16[256,2048]{1,0:T(8,128)(2,1)} %get-tuple-element.51), channel_id=1, source_target_pairs={{0,1},{1,0},{2,3},{3,2},{4,5},{5,4},{6,7},{7,6},{8,9},{9,8},{10,11... | collective-permute-start | bytes 3145736 | tf_op jit(solution)/shard_map/ppermute | solution.py:477
  56.2 11.4 %collective-permute-start.21 = (bf16[64,512]{1,0:T(8,128)(2,1)S(1)}, bf16[64,512]{1,0:T(8,128)(2,1)S(1)}, u32[]{:S(2)}, u32[]{:S(2)}) collective-permute-start(bf16[64,512]{1,0:T(8,128)(2,1)S(1)} %get-tuple-element.73), channel_id=1, source_target_pairs={{0,4},{1,5},{2,6},{3,7},{4,0},{5,1},{6,2},{7,3},{8,12},{9,13},{10,... | collective-permute-start | bytes 196616 | tf_op jit(solution)/shard_map/ppermute | solution.py:482
  63.3 6.6 %collective-permute-start.22 = (bf16[64,512]{1,0:T(8,128)(2,1)S(1)}, bf16[64,512]{1,0:T(8,128)(2,1)S(1)}, u32[]{:S(2)}, u32[]{:S(2)}) collective-permute-start(bf16[64,512]{1,0:T(8,128)(2,1)S(1)} %get-tuple-element.74), channel_id=1, source_target_pairs={{0,6},{1,7},{2,4},{3,5},{4,2},{5,3},{6,0},{7,1},{8,14},{9,15},{10,... | collective-permute-start | bytes 196616 | tf_op jit(solution)/shard_map/ppermute | solution.py:482
  63.8 6.4 %collective-permute-start.19 = (bf16[64,512]{1,0:T(8,128)(2,1)S(1)}, bf16[64,512]{1,0:T(8,128)(2,1)S(1)}, u32[]{:S(2)}, u32[]{:S(2)}) collective-permute-start(bf16[64,512]{1,0:T(8,128)(2,1)S(1)} %slice.67), channel_id=1, source_target_pairs={{0,2},{1,3},{2,0},{3,1},{4,6},{5,7},{6,4},{7,5},{8,10},{9,11},{10,... | collective-permute-start | bytes 196616 | tf_op jit(solution)/shard_map/ppermute | solution.py:482
  71.7 7.2 %collective-permute-start.24 = (bf16[64,512]{1,0:T(8,128)(2,1)S(1)}, bf16[64,512]{1,0:T(8,128)(2,1)S(1)}, u32[]{:S(2)}, u32[]{:S(2)}) collective-permute-start(bf16[64,512]{1,0:T(8,128)(2,1)S(1)} %fusion.8), channel_id=1, source_target_pairs={{0,4},{1,5},{2,6},{3,7},{4,0},{5,1},{6,2},{7,3},{8,12},{9,13},{10,... | collective-permute-start | bytes 196616 | tf_op jit(solution)/shard_map/ppermute | solution.py:482
  73.7 6.2 %collective-permute-start.25 = (bf16[64,512]{1,0:T(8,128)(2,1)S(1)}, bf16[64,512]{1,0:T(8,128)(2,1)S(1)}, u32[]{:S(2)}, u32[]{:S(2)}) collective-permute-start(bf16[64,512]{1,0:T(8,128)(2,1)S(1)} %fusion.8), channel_id=1, source_target_pairs={{0,6},{1,7},{2,4},{3,5},{4,2},{5,3},{6,0},{7,1},{8,14},{9,15},{10,... | collective-permute-start | bytes 196616 | tf_op jit(solution)/shard_map/ppermute | solution.py:482
  79.9 9.2 %collective-permute-start.26 = (bf16[256,512]{1,0:T(8,128)(2,1)S(1)}, bf16[256,512]{1,0:T(8,128)(2,1)S(1)}, u32[]{:S(2)}, u32[]{:S(2)}) collective-permute-start(bf16[256,512]{1,0:T(8,128)(2,1)S(1)} %pad_maximum_fusion.refs_0_), channel_id=1, source_target_pairs={{0,8},{8,0},{16,24},{24,16},{1,9},{9,1},{17,25},{25,17},{2,10},{10... | collective-permute-start | bytes 786440 | tf_op jit(solution)/shard_map/ppermute | solution.py:486
  81.5 8.1 %collective-permute-start.27 = (bf16[256,512]{1,0:T(8,128)(2,1)S(1)}, bf16[256,512]{1,0:T(8,128)(2,1)S(1)}, u32[]{:S(2)}, u32[]{:S(2)}) collective-permute-start(bf16[256,512]{1,0:T(8,128)(2,1)S(1)} %pad_maximum_fusion.refs_0_), channel_id=1, source_target_pairs={{0,16},{8,24},{16,0},{24,8},{1,17},{9,25},{17,1},{25,9},{2,18},{10... | collective-permute-start | bytes 786440 | tf_op jit(solution)/shard_map/ppermute | solution.py:486
  84.7 11.0 %collective-permute-start.10 = (bf16[64,2048]{1,0:T(8,128)(2,1)S(1)}, bf16[64,2048]{1,0:T(8,128)(2,1)S(1)}, u32[]{:S(2)}, u32[]{:S(2)}) collective-permute-start(bf16[64,2048]{1,0:T(8,128)(2,1)S(1)} %get-tuple-element.71), channel_id=1, source_target_pairs={{0,6},{1,7},{2,4},{3,5},{4,2},{5,3},{6,0},{7,1},{8,14},{9,15},{10,... | collective-permute-start | bytes 786440 | tf_op jit(solution)/shard_map/ppermute | solution.py:482
  86.5 14.6 %collective-permute-start.8 = (bf16[64,2048]{1,0:T(8,128)(2,1)S(1)}, bf16[64,2048]{1,0:T(8,128)(2,1)S(1)}, u32[]{:S(2)}, u32[]{:S(2)}) collective-permute-start(bf16[64,2048]{1,0:T(8,128)(2,1)S(1)} %get-tuple-element.70), channel_id=1, source_target_pairs={{0,2},{1,3},{2,0},{3,1},{4,6},{5,7},{6,4},{7,5},{8,10},{9,11},{10,... | collective-permute-start | bytes 786440 | tf_op jit(solution)/shard_map/ppermute | solution.py:482
  86.8 26.7 %collective-permute-start.9 = (bf16[64,2048]{1,0:T(8,128)(2,1)S(1)}, bf16[64,2048]{1,0:T(8,128)(2,1)S(1)}, u32[]{:S(2)}, u32[]{:S(2)}) collective-permute-start(bf16[64,2048]{1,0:T(8,128)(2,1)S(1)} %get-tuple-element.72), channel_id=1, source_target_pairs={{0,4},{1,5},{2,6},{3,7},{4,0},{5,1},{6,2},{7,3},{8,12},{9,13},{10,... | collective-permute-start | bytes 786440 | tf_op jit(solution)/shard_map/ppermute | solution.py:482
  89.2 24.5 %collective-permute-start.28 = (bf16[256,512]{1,0:T(8,128)(2,1)S(1)}, bf16[256,512]{1,0:T(8,128)(2,1)S(1)}, u32[]{:S(2)}, u32[]{:S(2)}) collective-permute-start(bf16[256,512]{1,0:T(8,128)(2,1)S(1)} %pad_maximum_fusion.refs_0_), channel_id=1, source_target_pairs={{0,24},{8,16},{16,8},{24,0},{1,25},{9,17},{17,9},{25,1},{2,26},{10... | collective-permute-start | bytes 786440 | tf_op jit(solution)/shard_map/ppermute | solution.py:486
  89.6 26.9 %collective-permute-start.29 = (bf16[256,512]{1,0:T(8,128)(2,1)S(1)}, bf16[256,512]{1,0:T(8,128)(2,1)S(1)}, u32[]{:S(2)}, u32[]{:S(2)}) collective-permute-start(bf16[256,512]{1,0:T(8,128)(2,1)S(1)} %pad_maximum_fusion.refs_0_), channel_id=1, source_target_pairs={{0,1},{1,0},{2,3},{3,2},{4,5},{5,4},{6,7},{7,6},{8,9},{9,8},{10,11... | collective-permute-start | bytes 786440 | tf_op jit(solution)/shard_map/ppermute | solution.py:477
  95.7 22.3 %collective-permute-start.30 = (bf16[256,512]{1,0:T(8,128)(2,1)S(1)}, bf16[256,512]{1,0:T(8,128)(2,1)S(1)}, u32[]{:S(2)}, u32[]{:S(2)}) collective-permute-start(bf16[256,512]{1,0:T(8,128)(2,1)S(1)} %collective-permute-done.26.refs_1_), channel_id=1, source_target_pairs={{0,1},{1,0},{2,3},{3,2},{4,5},{5,4},{6,7},{7,6},{8,9},{9,8},{10,11... | collective-permute-start | bytes 786440 | tf_op jit(solution)/shard_map/ppermute | solution.py:477
  101.1 17.0 %collective-permute-start.31 = (bf16[256,512]{1,0:T(8,128)(2,1)S(1)}, bf16[256,512]{1,0:T(8,128)(2,1)S(1)}, u32[]{:S(2)}, u32[]{:S(2)}) collective-permute-start(bf16[256,512]{1,0:T(8,128)(2,1)S(1)} %collective-permute-done.27.refs_2_), channel_id=1, source_target_pairs={{0,1},{1,0},{2,3},{3,2},{4,5},{5,4},{6,7},{7,6},{8,9},{9,8},{10,11... | collective-permute-start | bytes 786440 | tf_op jit(solution)/shard_map/ppermute | solution.py:477
  113.6 8.6 %collective-permute-start.11 = (bf16[64,2048]{1,0:T(8,128)(2,1)S(1)}, bf16[64,2048]{1,0:T(8,128)(2,1)S(1)}, u32[]{:S(2)}, u32[]{:S(2)}) collective-permute-start(bf16[64,2048]{1,0:T(8,128)(2,1)S(1)} %fusion.3.refs_0_), channel_id=1, source_target_pairs={{0,2},{1,3},{2,0},{3,1},{4,6},{5,7},{6,4},{7,5},{8,10},{9,11},{10,... | collective-permute-start | bytes 786440 | tf_op jit(solution)/shard_map/ppermute | solution.py:482
  113.7 13.0 %collective-permute-start.14 = (bf16[64,2048]{1,0:T(8,128)(2,1)S(1)}, bf16[64,2048]{1,0:T(8,128)(2,1)S(1)}, u32[]{:S(2)}, u32[]{:S(2)}) collective-permute-start(bf16[64,2048]{1,0:T(8,128)(2,1)S(1)} %fusion.3.refs_0_), channel_id=1, source_target_pairs={{0,4},{1,5},{2,6},{3,7},{4,0},{5,1},{6,2},{7,3},{8,12},{9,13},{10,... | collective-permute-start | bytes 786440 | tf_op jit(solution)/shard_map/ppermute | solution.py:482
  116.6 10.1 %collective-permute-start.15 = (bf16[64,2048]{1,0:T(8,128)(2,1)S(1)}, bf16[64,2048]{1,0:T(8,128)(2,1)S(1)}, u32[]{:S(2)}, u32[]{:S(2)}) collective-permute-start(bf16[64,2048]{1,0:T(8,128)(2,1)S(1)} %fusion.3.refs_0_), channel_id=1, source_target_pairs={{0,6},{1,7},{2,4},{3,5},{4,2},{5,3},{6,0},{7,1},{8,14},{9,15},{10,... | collective-permute-start | bytes 786440 | tf_op jit(solution)/shard_map/ppermute | solution.py:482
  118.1 9.1 %collective-permute-start.32 = (bf16[256,512]{1,0:T(8,128)(2,1)S(1)}, bf16[256,512]{1,0:T(8,128)(2,1)S(1)}, u32[]{:S(2)}, u32[]{:S(2)}) collective-permute-start(bf16[256,512]{1,0:T(8,128)(2,1)S(1)} %collective-permute-done.28.refs_3_), channel_id=1, source_target_pairs={{0,1},{1,0},{2,3},{3,2},{4,5},{5,4},{6,7},{7,6},{8,9},{9,8},{10,11... | collective-permute-start | bytes 786440 | tf_op jit(solution)/shard_map/ppermute | solution.py:477
  118.1 30.0 %collective-permute-start.12 = (bf16[64,2048]{1,0:T(8,128)(2,1)S(1)}, bf16[64,2048]{1,0:T(8,128)(2,1)S(1)}, u32[]{:S(2)}, u32[]{:S(2)}) collective-permute-start(bf16[64,2048]{1,0:T(8,128)(2,1)S(1)} %fusion.3.refs_0_), channel_id=1, source_target_pairs={{0,1},{1,0},{2,3},{3,2},{4,5},{5,4},{6,7},{7,6},{8,9},{9,8},{10,11... | collective-permute-start | bytes 786440 | tf_op jit(solution)/shard_map/ppermute | solution.py:477
  122.2 25.8 %collective-permute-start.13 = (bf16[64,2048]{1,0:T(8,128)(2,1)S(1)}, bf16[64,2048]{1,0:T(8,128)(2,1)S(1)}, u32[]{:S(2)}, u32[]{:S(2)}) collective-permute-start(bf16[64,2048]{1,0:T(8,128)(2,1)S(1)} %collective-permute-done.11.refs_1_), channel_id=1, source_target_pairs={{0,1},{1,0},{2,3},{3,2},{4,5},{5,4},{6,7},{7,6},{8,9},{9,8},{10,11... | collective-permute-start | bytes 786440 | tf_op jit(solution)/shard_map/ppermute | solution.py:477
  126.7 21.4 %collective-permute-start.16 = (bf16[64,2048]{1,0:T(8,128)(2,1)S(1)}, bf16[64,2048]{1,0:T(8,128)(2,1)S(1)}, u32[]{:S(2)}, u32[]{:S(2)}) collective-permute-start(bf16[64,2048]{1,0:T(8,128)(2,1)S(1)} %collective-permute-done.14.refs_4_), channel_id=1, source_target_pairs={{0,1},{1,0},{2,3},{3,2},{4,5},{5,4},{6,7},{7,6},{8,9},{9,8},{10,11... | collective-permute-start | bytes 786440 | tf_op jit(solution)/shard_map/ppermute | solution.py:477
  126.7 21.4 %collective-permute-start.17 = (bf16[64,2048]{1,0:T(8,128)(2,1)S(1)}, bf16[64,2048]{1,0:T(8,128)(2,1)S(1)}, u32[]{:S(2)}, u32[]{:S(2)}) collective-permute-start(bf16[64,2048]{1,0:T(8,128)(2,1)S(1)} %collective-permute-done.15.refs_5_), channel_id=1, source_target_pairs={{0,1},{1,0},{2,3},{3,2},{4,5},{5,4},{6,7},{7,6},{8,9},{9,8},{10,11... | collective-permute-start | bytes 786440 | tf_op jit(solution)/shard_map/ppermute | solution.py:477
  159.6 5.5 %collective-permute-start.34 = (f32[48,320]{1,0:T(8,128)S(1)}, f32[48,320]{1,0:T(8,128)S(1)}, u32[]{:S(2)}, u32[]{:S(2)}) collective-permute-start(f32[48,320]{1,0:T(8,128)S(1)} %shard_map.109.a), channel_id=1, source_target_pairs={{0,16},{8,24},{16,0},{24,8},{1,17},{9,25},{17,1},{25,9},{2,18},{10... | collective-permute-start | bytes 184328 | tf_op jit(solution)/shard_map/ppermute | solution.py:486
  161.7 5.3 %collective-permute-start.35 = (f32[48,320]{1,0:T(8,128)S(1)}, f32[48,320]{1,0:T(8,128)S(1)}, u32[]{:S(2)}, u32[]{:S(2)}) collective-permute-start(f32[48,320]{1,0:T(8,128)S(1)} %shard_map.109.a), channel_id=1, source_target_pairs={{0,24},{8,16},{16,8},{24,0},{1,25},{9,17},{17,9},{25,1},{2,26},{10... | collective-permute-start | bytes 184328 | tf_op jit(solution)/shard_map/ppermute | solution.py:486
  (25 other events, 199.7 us)
where the time goes:
time: 183 us; the launch traced here: 182 us
  Pallas kernels  72.6 us (40%)
  waiting for transfers between devices  64.2 us (35%)
  starting transfers between devices  36.9 us (20%)
  local copies, waits for them, and re-layouts  4.19 us (2%)
  other arithmetic  2.71 us (1%)
    pallas_call x9, Pallas kernels, call(): pl.pallas_call(body, grid=grid, in_specs=in_specs, out_specs=out_specs, o...  72.6 us
    ppermute x15, waiting for transfers between devices, to_chip(): return lax.ppermute(x, 'mp', pairs)  59.3 us
    ppermute x15, starting transfers between devices, to_chip(): return lax.ppermute(x, 'mp', pairs)  26.9 us
    ppermute x6, starting transfers between devices, to_probe(): return lax.ppermute(x, 'probe', [(i, i ^ flip) for i in range(probes)])  7.44 us
    unnamed x42, local copies, waits for them, and re-layouts  4.1 us
    ppermute x6, waiting for transfers between devices, to_probe(): return lax.ppermute(x, 'probe', [(i, i ^ flip) for i in range(probes)])  4.01 us
  transfers between devices with their start and end apart: 36, of which 17 were waited for; matrix products, arithmetic and copies ran while one was open for 2% of the time, Pallas kernels for 26%

commit v1 on v0

v1 whole, which is shorter than its diff:
```python
import functools
import math

import jax
import jax.numpy as jnp
from jax import lax
from jax.experimental import pallas as pl
from jax.experimental.pallas import tpu as pltpu
from jax.sharding import PartitionSpec as P


BLOCK_ROWS = 2
BLOCK_COLS = 128
STEP = 4

beta_one = 0.9
beta_two = 0.999
epsilon = 0.0001
root_half = 0.7978845608028654
cubic = 0.044715

F32 = jnp.float32
BF16 = jnp.bfloat16


def gelu_parts(value):
    square = value * value
    inner = root_half * (value + cubic * square * value)
    slope_inner = root_half * (1.0 + 3.0 * cubic * square)
    curve_inner = 6.0 * root_half * cubic * value
    tangent = jnp.tanh(inner)
    damping = 1.0 - tangent * tangent
    activated = 0.5 * value * (1.0 + tangent)
    slope = 0.5 * (1.0 + tangent) + 0.5 * value * damping * slope_inner
    bend = damping * slope_inner + 0.5 * value * damping * (
        curve_inner - 2.0 * tangent * slope_inner * slope_inner
    )
    return (activated, slope, bend)


def dot_nt(left, right):
    return lax.dot_general(left, right, (((1,), (1,)), ((), ())), preferred_element_type=F32)


def dot_tn(left, right):
    return lax.dot_general(left, right, (((0,), (0,)), ((), ())), preferred_element_type=F32)


def dot_nn(left, right):
    return jnp.dot(left, right, preferred_element_type=F32)


FORWARD_UNITS = 320
TILT_UNITS = 320
SPREAD_COLS = 512
BASE_UNITS = 160
TANGENT_UNITS = 320
UPDATE_UNITS = 320
FORWARD_LIMIT = 24
BASE_LIMIT = 28
TANGENT_LIMIT = 32
UPDATE_LIMIT = 16


def unit_block(units, wanted):
    return wanted if units % wanted == 0 else units


def whole(shape):
    zeros = (0,) * len(shape)
    return pl.BlockSpec(shape, lambda *_: zeros, pipeline_mode=pl.Buffered(1))


def in_vmem(array):
    return pltpu.with_memory_space_constraint(array, pltpu.VMEM)


def in_hbm(array):
    return pltpu.with_memory_space_constraint(array, pltpu.HBM)


HELD = pl.BlockSpec(memory_space=pltpu.VMEM)


def call(body, grid, in_specs, out_specs, out_shape, scratch, flops, traffic, limit, args, aliases={}):
    return pl.pallas_call(
        body,
        grid=grid,
        in_specs=in_specs,
        out_specs=out_specs,
        out_shape=out_shape,
        scratch_shapes=scratch,
        input_output_aliases=aliases,
        compiler_params=pltpu.CompilerParams(
            dimension_semantics=("arbitrary",) * len(grid), vmem_limit_bytes=limit * 1024 * 1024
        ),
        cost_estimate=pl.CostEstimate(flops=flops, bytes_accessed=traffic, transcendentals=0),
    )(*args)


def column_sums(values, kind, out):
    rows, width = values.shape
    lanes = lax.broadcasted_iota(jnp.int32, (rows, 128), 1)
    cols = width // BLOCK_COLS
    for at in range(cols):
        part = values[:, at * BLOCK_COLS : (at + 1) * BLOCK_COLS]
        out = jnp.where(lanes == kind * cols + at, jnp.sum(part, axis=1, keepdims=True), out)
    return out


def norm_kernel(tokens, gain, out):
    x = tokens[...].astype(F32)
    factor = lax.rsqrt(jnp.mean(x * x, axis=-1, keepdims=True) + 1e-06)
    out[...] = (x * factor * gain[...]).astype(BF16)


def norm(tokens, gain):
    rows, width = tokens.shape
    return call(
        norm_kernel,
        (1,),
        [whole((rows, width)), whole((1, width))],
        whole((rows, width)),
        jax.ShapeDtypeStruct((rows, width), BF16),
        [],
        rows * width * 4,
        rows * width * 4,
        8,
        (in_hbm(tokens), in_hbm(gain.reshape(1, width))),
    )


def joined(refs):
    return jnp.concatenate([ref[...] for ref in refs], axis=1)


def forward_kernel(pieces, chunk, refs):
    blocks = refs[:pieces]
    w = refs[pieces]
    (x, p_out, g_out, s_out, b_out, hid_out, own_q, sib_q, acc_q) = refs[-9:]
    step = pl.program_id(0)
    rows = blocks[0].shape[0]
    count = rows * pieces
    first_row = chunk * count

    @pl.when(step == 0)
    def _():
        for at in range(pieces):
            x[first_row + at * rows : first_row + (at + 1) * rows] = blocks[at][...]

    total, width = w.shape[1:]
    units = unit_block(total, FORWARD_UNITS)
    span = pl.ds(pl.multiple_of(step * units, 16), units)
    pre = dot_nt(w[0:2, span].reshape(2 * units, width), x[first_row : first_row + count])
    pre_gate, pre_up = (pre[:units], pre[units:])
    activated, slope, bend = gelu_parts(pre_gate)
    p_out[span] = pre_up * slope
    g_out[span] = activated
    s_out[span] = slope
    b_out[span] = pre_up * bend
    hidden = (activated * pre_up).astype(BF16)
    hid_out[span] = hidden
    quarter = acc_q.shape[1]
    first = pl.multiple_of(lax.axis_index("probe") * quarter, quarter)
    add_q = dot_tn(hidden, w[2, span, pl.ds(first, quarter)])

    @pl.when(step == 0)
    def _():
        acc_q[...] = add_q

    @pl.when(step > 0)
    def _():
        acc_q[...] += add_q

    @pl.when(step == pl.num_programs(0) - 1)
    def _():
        half = own_q.shape[0]
        own_q[...] = acc_q[:half]
        sib_q[...] = acc_q[half:].astype(sib_q.dtype)


def forward(blocks, weights, chunk, chunks, x, quarter, sib_type):
    rows, width = blocks[0].shape
    count = rows * len(blocks)
    units = weights.shape[1]
    ub = unit_block(units, FORWARD_UNITS)
    half = count // 2
    held = [] if x is None else [x]
    return call(
        lambda *refs: forward_kernel(len(blocks), chunk, refs),
        (units // ub,),
        [whole((rows, width))] * len(blocks) + [HELD] * (1 + len(held)),
        [HELD] * 8,
        [pltpu.VMEM((count * chunks, width), BF16)]
        + [pltpu.VMEM((units, count), F32)] * 4
        + [
            pltpu.VMEM((units, count), BF16),
            pltpu.VMEM((half, quarter), F32),
            pltpu.VMEM((half, quarter), sib_type),
        ],
        [pltpu.VMEM((count, quarter), F32)],
        2 * count * units * width * 2,
        units * width * 6 + units * count * 18 + count * width * 4,
        FORWARD_LIMIT,
        (*blocks, in_vmem(weights), *map(in_vmem, held)),
        {len(blocks) + 1: 0} if held else {},
    )


def tilt_kernel(chunk, z, x, p, g, s, b, q_out, s_out, tan_out):
    total, width = z.shape[1:]
    units = unit_block(total, TILT_UNITS)
    count = p.shape[1]
    span = pl.ds(pl.multiple_of(pl.program_id(0) * units, 16), units)
    rows = slice(chunk * count, (chunk + 1) * count)
    tan = dot_nt(z[0:2, span].reshape(2 * units, width), x[rows])
    tan_gate, tan_up = (tan[:units], tan[units:])
    slope = s[span]
    q_out[span] = tan_up * slope + b[span] * tan_gate
    s_out[span] = slope * tan_gate
    tan_out[span] = (p[span] * tan_gate + g[span] * tan_up).astype(BF16)


def tilt(signs, chunk, x, p, g, s, b):
    units, count = p.shape
    width = x.shape[1]
    ub = unit_block(units, TILT_UNITS)
    return call(
        functools.partial(tilt_kernel, chunk),
        (units // ub,),
        [HELD] * 6,
        [HELD] * 3,
        [pltpu.VMEM((units, count), F32)] * 2 + [pltpu.VMEM((units, count), BF16)],
        [],
        2 * count * units * width * 2,
        units * width * 4 + units * count * 26 + count * width * 2,
        FORWARD_LIMIT,
        tuple(map(in_vmem, (signs, x, p, g, s, b))),
    )


def spread_kernel(parts, refs):
    (w, z) = refs[:2]
    tans = refs[2 : 2 + parts]
    hids = refs[2 + parts : 2 + 2 * parts]
    (own, sib, left) = refs[2 + 2 * parts :]
    units, count = hids[0].shape
    step = pl.program_id(0)

    @pl.when(step == 0)
    def _():
        for at in range(parts):
            span = slice(at * count, (at + 1) * count)
            left[span, :units] = tans[at][...].T
            left[span, units:] = hids[at][...].T

    cols = min(SPREAD_COLS, own.shape[1])
    span = pl.ds(pl.multiple_of(step * cols, cols), cols)
    total = dot_nn(left[...], jnp.concatenate([w[2, :, span], z[2, :, span]], axis=0))
    half = count // 2
    for at in range(parts):
        top = at * count
        rows = slice(at * half, (at + 1) * half)
        own[rows, span] = total[top : top + half]
        sib[rows, span] = total[top + half : top + count].astype(sib.dtype)


def spread(weights, signs, tans, hids, sib_type):
    units, count = hids[0].shape
    parts = len(hids)
    width = weights.shape[2]
    half = parts * count // 2
    cols = SPREAD_COLS
    return call(
        lambda *refs: spread_kernel(parts, refs),
        (width // cols,),
        [HELD] * (2 + 2 * parts),
        [HELD, HELD],
        [pltpu.VMEM((half, width), F32), pltpu.VMEM((half, width), sib_type)],
        [pltpu.VMEM((parts * count, 2 * units), BF16)],
        4 * parts * count * units * width,
        units * width * 4 + half * width * 6,
        FORWARD_LIMIT,
        tuple(map(in_vmem, (weights, signs, *tans, *hids))),
    )


def fold_kernel(parts, rows, refs):
    owns = refs[:parts]
    gots = refs[parts : 2 * parts]
    outs = refs[2 * parts :]
    at = 0
    for own, got in zip(owns, gots):
        for first in range(0, own.shape[0], rows):
            span = slice(first, first + rows)
            outs[at][...] = (own[span] + got[span].astype(F32)).astype(outs[at].dtype)
            at += 1


def fold(owns, gots, rows):
    parts = len(owns)
    blocks = sum(own.shape[0] for own in owns) // rows
    width = owns[0].shape[1]
    return call(
        lambda *refs: fold_kernel(parts, rows, refs),
        (1,),
        [HELD] * (2 * parts),
        [HELD] * blocks,
        [pltpu.VMEM((rows, width), F32)] + [pltpu.VMEM((rows, width), BF16)] * (blocks - 1),
        [],
        rows * blocks * width * 64,
        rows * blocks * width * 8,
        8,
        tuple(map(in_vmem, (*owns, *gots))),
    )


def load_kernel(plan, refs):
    count = len(plan)
    (sources, targets, sems) = (refs[:count], refs[count : 2 * count], refs[2 * count])
    copies = []
    for source, target, picks in zip(sources, targets, plan):
        for place, pick in enumerate(picks):
            copies.append(
                pltpu.make_async_copy(source.at[pick], target.at[place], sems.at[len(copies)])
            )
    for copy in copies:
        copy.start()
    for copy in copies:
        copy.wait()


def load(arrays, plan):
    shapes = [(len(picks), *array.shape[1:]) for array, picks in zip(arrays, plan)]
    size = sum(math.prod(dims) for dims in shapes)
    return pl.pallas_call(
        lambda *refs: load_kernel(plan, refs),
        name="load",
        in_specs=[pl.BlockSpec(memory_space=pltpu.HBM)] * len(arrays),
        out_specs=[HELD] * len(arrays),
        out_shape=[pltpu.VMEM(dims, array.dtype) for dims, array in zip(shapes, arrays)],
        scratch_shapes=[pltpu.SemaphoreType.DMA((sum(map(len, plan)),))],
        compiler_params=pltpu.CompilerParams(vmem_limit_bytes=8 * 1024 * 1024),
        cost_estimate=pl.CostEstimate(
            flops=size * 64, bytes_accessed=size * 8, transcendentals=0
        ),
    )(*map(in_hbm, arrays))


def load_moment(array):
    kinds, units, width = array.shape
    ub = unit_block(units, BASE_UNITS)
    split = array.reshape(kinds * units // ub, ub, width)
    return load([split], [tuple(range(split.shape[0]))])[0]


def load_weights(weights, signs):
    kinds, units, width = weights.shape
    halves = 2 if units % 32 == 0 else 1
    dims = (kinds * halves, units // halves, width)
    picks = tuple(range(kinds * halves))
    loaded = load([weights.reshape(dims), signs.reshape(dims)], [picks, picks])
    return [array.reshape(kinds, units, width) for array in loaded]


def joined(refs, span):
    return jnp.concatenate([ref[span] for ref in refs], axis=1)


def base_kernel(pieces, parts, refs):
    blocks = refs[: 2 * pieces]
    refs = refs[2 * pieces :]
    (w, z, m, normed) = refs[:4]
    groups = [refs[4 + at * parts : 4 + (at + 1) * parts] for at in range(6)]
    (ps, gs, qs, ss, hids, tans) = groups
    (new_m, held, e_gate, e_up, sums, dout) = refs[4 + 6 * parts :]
    step = pl.program_id(0)
    half, quarter = blocks[0].shape
    chunk = 2 * half // parts

    @pl.when(step == 0)
    def _():
        me = lax.axis_index("probe")
        for at in range(pieces):
            first = pl.multiple_of((me ^ at) * quarter, quarter)
            for side in range(2):
                source = blocks[side * pieces + at]
                for part in range(parts):
                    start = part * chunk + side * (chunk // 2)
                    dout[start : start + chunk // 2, pl.ds(first, quarter)] = source[
                        part * (chunk // 2) : (part + 1) * (chunk // 2)
                    ]

    units = w.shape[1]
    kinds = new_m.shape[0]
    blocks_of = m.shape[0] // kinds
    span = pl.ds(pl.multiple_of(step * units, 16), units)
    d = dout[...]
    both = dot_nt(jnp.concatenate([w[0], z[0, 0]], axis=0), d)
    dhid, sdhid = (both[:units], both[units:])
    pv, gv = (joined(ps, span), joined(gs, span))
    e_gate[span] = sdhid * pv + dhid * joined(qs, span)
    e_up[span] = sdhid * gv + dhid * joined(ss, span)
    inner = jnp.concatenate([(dhid * pv).astype(BF16), (dhid * gv).astype(BF16)], axis=0)
    grads = dot_nn(inner, normed[...])

    def moment(kind, grad):
        at = kind * blocks_of + step
        value = beta_one * m[at] + (1.0 - beta_one) * grad
        new_m[kind] = value
        held[at] = value

    moment(0, grads[:units])
    moment(1, grads[units:])
    outer = dot_nn(jnp.concatenate([joined(hids, span), joined(tans, span)], axis=0), d)
    moment(2, outer[:units])
    sums[span] = column_sums(z[0, 0].astype(F32) * outer[units:], 2, jnp.zeros((units, 128), F32))


def base(pieces, weights, signs, m, x, ps, gs, qs, ss, hids, tans):
    half, quarter = pieces[0].shape
    kinds, units, width = weights.shape
    count = 2 * half
    parts = len(ps)
    ub = unit_block(units, BASE_UNITS)
    return call(
        lambda *refs: base_kernel(len(pieces) // 2, parts, refs),
        (units // ub,),
        [whole((half, quarter))] * len(pieces)
        + [
            pl.BlockSpec((1, ub, width), lambda i: (2, i, 0)),
            pl.BlockSpec((1, 1, ub, width), lambda i: (0, 2, i, 0)),
        ]
        + [HELD] * (2 + 6 * parts),
        [pl.BlockSpec((kinds, ub, width), lambda i: (0, i, 0))] + [HELD] * 4,
        [
            jax.ShapeDtypeStruct((kinds, units, width), F32),
            pltpu.VMEM(m.shape, F32),
            pltpu.VMEM((units, count), F32),
            pltpu.VMEM((units, count), F32),
            pltpu.VMEM((units, 128), F32),
        ],
        [pltpu.VMEM((count, width), BF16)],
        2 * count * units * width * 6,
        units * width * 28 + units * count * 28,
        BASE_LIMIT,
        (
            *pieces,
            in_hbm(weights),
            in_hbm(signs),
            *map(in_vmem, (m, x, *ps, *gs, *qs, *ss, *hids, *tans)),
        ),
        {len(pieces) + 2: 1},
    )


def tangent_kernel(pieces, parts, refs):
    blocks = refs[:pieces]
    (w, z, normed, e_gate, e_up, sums_in) = refs[pieces : pieces + 6]
    refs = refs[pieces + 6 :]
    (ps, gs, hids) = [refs[at * parts : (at + 1) * parts] for at in range(3)]
    (sums, tdout, rows_sum, pairs) = refs[3 * parts :]
    step = pl.program_id(0)
    rows = blocks[0].shape[0]

    @pl.when(step == 0)
    def _():
        for at in range(pieces):
            tdout[at * rows : (at + 1) * rows] = blocks[at][...]

    units = w.shape[1]
    span = pl.ds(pl.multiple_of(step * units, 16), units)
    t = tdout[...]
    tdh = dot_nt(w[0], t)
    inner = jnp.concatenate(
        [
            (tdh * joined(ps, span) + e_gate[span]).astype(BF16),
            (tdh * joined(gs, span) + e_up[span]).astype(BF16),
        ],
        axis=0,
    )
    hv = dot_nn(inner, normed[...])
    hv_out = dot_nn(joined(hids, span), t)
    made = jnp.zeros((units, 128), F32)
    made = column_sums(z[0, 0].astype(F32) * hv[:units], 0, made)
    made = column_sums(z[0, 1].astype(F32) * hv[units:], 1, made)
    made = column_sums(z[0, 2].astype(F32) * hv_out, 2, made)
    rows_sum[...] = made + sums_in[span]
    half = units // BLOCK_ROWS
    pairs[pl.ds(pl.multiple_of(step * half, 8), half), :] = (
        rows_sum[pl.ds(0, half, stride=2), :] + rows_sum[pl.ds(1, half, stride=2), :]
    )

    @pl.when(step == pl.num_programs(0) - 1)
    def _():
        sums[...] = pairs[...].T[: sums.shape[0]]


def tangent(blocks, weights, signs, normed, e_gate, e_up, sums, ps, gs, hids):
    rows, width = blocks[0].shape
    count = normed.shape[0]
    kinds, units, _ = weights.shape
    parts = len(ps)
    ub = unit_block(units, TANGENT_UNITS)
    cols = width // BLOCK_COLS
    return call(
        lambda *refs: tangent_kernel(len(blocks), parts, refs),
        (units // ub,),
        [whole((rows, width))] * len(blocks)
        + [
            pl.BlockSpec((1, ub, width), lambda i: (2, i, 0)),
            pl.BlockSpec((1, kinds, ub, width), lambda i: (0, 0, i, 0)),
        ]
        + [HELD] * (4 + 3 * parts),
        whole((kinds * cols, units // BLOCK_ROWS)),
        jax.ShapeDtypeStruct((kinds * cols, units // BLOCK_ROWS), F32),
        [
            pltpu.VMEM((count, width), BF16),
            pltpu.VMEM((ub, 128), F32),
            pltpu.VMEM((units // BLOCK_ROWS, 128), F32),
        ],
        2 * count * units * width * 4,
        units * width * 8 + units * count * 18,
        TANGENT_LIMIT,
        (
            *blocks,
            in_hbm(weights),
            in_hbm(signs),
            *map(in_vmem, (normed, e_gate, e_up, sums, *ps, *gs, *hids)),
        ),
    )


def update_kernel(probes, a, b, c, d, v, m, hess, new_v, update, scales):
    kinds, cols, half = v.shape
    kind, step = (pl.program_id(0), pl.program_id(1))

    @pl.when((kind == 0) & (step == 0))
    def _():
        total = (a[...] + b[...]) + (c[...] + d[...])
        for at in range(kinds):
            h = total[at * cols : (at + 1) * cols] * (1.0 / (BLOCK_ROWS * BLOCK_COLS * probes))
            hess[at] = h
            nv = beta_two * v[at] + (1.0 - beta_two) * h * h
            new_v[at] = nv
            denom = jnp.sqrt(nv / (1.0 - beta_two**STEP)) + epsilon
            scale = 1.0 / (denom * (1.0 - beta_one**STEP))
            wide = jnp.concatenate([scale, jnp.zeros((128 - cols, half), F32)], axis=0).T
            scales[at, pl.ds(0, half, stride=2), :] = wide
            scales[at, pl.ds(1, half, stride=2), :] = wide

    tall = update.shape[1]
    full = scales[kind, pl.ds(pl.multiple_of(step * tall, tall), tall), :]
    pieces = tall // m.shape[1]
    first = (kind * pl.num_programs(1) + step) * pieces
    for piece in range(pieces):
        rows = slice(piece * m.shape[1], (piece + 1) * m.shape[1])
        for at in range(cols):
            span = slice(at * BLOCK_COLS, (at + 1) * BLOCK_COLS)
            update[0, rows, span] = m[first + piece, :, span] * full[rows, at : at + 1]


def update_step(sums, v, m):
    kinds, _, half = v.shape
    units, width = (half * BLOCK_ROWS, m.shape[2])
    ub = unit_block(units, UPDATE_UNITS)
    m_spec = pl.BlockSpec((1, ub, width), lambda k, i: (k, i, 0))
    shape = jax.ShapeDtypeStruct
    return call(
        functools.partial(update_kernel, len(sums)),
        (kinds, units // ub),
        [whole(sums[0].shape)] * 4 + [whole(v.shape), pl.BlockSpec(memory_space=pltpu.VMEM)],
        [whole(v.shape), whole(v.shape), m_spec],
        [shape(v.shape, F32), shape(v.shape, F32), shape((kinds, units, width), F32)],
        [pltpu.VMEM((kinds, units, 128), F32)],
        units * width * 6,
        units * width * 24,
        UPDATE_LIMIT,
        (*sums, v, in_vmem(m)),
    )


def to_sibling(x, chips):
    return lax.ppermute(x, "mp", [(i, i ^ 1) for i in range(2 * chips)])


def to_chip(x, chips, flip):
    pairs = [(2 * z + c, 2 * (z ^ flip) + c) for z in range(chips) for c in range(2)]
    return lax.ppermute(x, "mp", pairs)


def to_probe(x, probes, flip):
    return lax.ppermute(x, "probe", [(i, i ^ flip) for i in range(probes)])


def gather_rows(x, chips):
    own = [x]
    for flip in range(1, chips):
        own.append(to_chip(x, chips, flip))
    sib = []
    for flip in range(chips):
        sib.append(to_sibling(own[flip], chips))
    half = chips // 2
    return [own[:half] + sib[:half], own[half:] + sib[half:]]


def near_path(normed, offset, weights, probe_signs, m_state, chips, probes):
    rows, width = normed.shape
    count = 2 * chips * rows
    quarter = width // probes
    chunks = gather_rows(normed, chips)
    w, z = load_weights(weights, probe_signs)
    x = None
    ps, gs, qs, ss, hids, tans, owns, gots = ([], [], [], [], [], [], [], [])
    for at, blocks in enumerate(chunks):
        x, p, g, s, b, hid, own_q, sib_q = forward(
            blocks, w, at, len(chunks), x, quarter, BF16
        )
        gots.append(to_sibling(sib_q, chips))
        owns.append(own_q)
        q, s, tan = tilt(z, at, x, p, g, s, b)
        for held, value in zip((ps, gs, qs, ss, hids, tans), (p, g, q, s, hid, tan)):
            held.append(value)
    own_t, sib_t = spread(w, z, tans, hids, BF16)
    kept, *sent = fold(owns, gots, rows)
    kept = kept + offset
    for flip in range(1, chips):
        kept = kept + to_chip(sent[flip - 1], chips, flip).astype(F32)
    part = (kept / count).astype(BF16)
    mine = [part]
    for flip in range(1, chips):
        mine.append(to_chip(part, chips, flip))
    mine = jnp.concatenate(mine, axis=0)
    pieces = [mine]
    for flip in range(1, probes):
        pieces.append(to_probe(mine, probes, flip))
    for at in range(probes):
        pieces.append(to_sibling(pieces[at], chips))
    got = to_sibling(sib_t, chips)
    kept, *sent = fold([own_t], [got], rows)
    for flip in range(1, chips):
        kept = kept + to_chip(sent[flip - 1], chips, flip).astype(F32)
    tan_dout = (kept / count).astype(BF16)
    tan_blocks = gather_rows(tan_dout, chips)
    held = load_moment(m_state)
    new_m, held, e_gate, e_up, sums = base(
        pieces, weights, probe_signs, held, x, ps, gs, qs, ss, hids, tans
    )
    sums = tangent(
        tan_blocks[0] + tan_blocks[1],
        weights,
        probe_signs,
        x,
        e_gate,
        e_up,
        sums,
        ps,
        gs,
        hids,
    )
    return new_m, held, sums


def far_path(normed, offset, weights, probe_signs, m_state, chips, probes):
    rows, width = normed.shape
    count = 2 * chips * rows
    quarter = width // probes
    blocks = [lax.all_gather(normed, "mp", axis=0, tiled=True)]
    w, z = load_weights(weights, probe_signs)
    x, p, g, s, b, hid, own_q, sib_q = forward(blocks, w, 0, 1, None, quarter, F32)
    q, s, tan = tilt(z, 0, x, p, g, s, b)
    own_t, sib_t = spread(w, z, [tan], [hid], F32)
    part = lax.psum_scatter(
        jnp.concatenate([own_q, sib_q], axis=0), "mp", scatter_dimension=0, tiled=True
    )
    mine = lax.all_gather(
        ((part + offset) / count).astype(BF16), "mp", axis=0, tiled=True
    )
    pieces = [mine] + [to_probe(mine, probes, flip) for flip in range(1, probes)]
    half = count // 2
    pieces = [piece[:half] for piece in pieces] + [piece[half:] for piece in pieces]
    kept = lax.psum_scatter(
        jnp.concatenate([own_t, sib_t], axis=0), "mp", scatter_dimension=0, tiled=True
    )
    tan_blocks = [lax.all_gather((kept / count).astype(BF16), "mp", axis=0, tiled=True)]
    held = load_moment(m_state)
    new_m, held, e_gate, e_up, sums = base(
        pieces, weights, probe_signs, held, x, [p], [g], [q], [s], [hid], [tan]
    )
    sums = tangent(
        tan_blocks, weights, probe_signs, x, e_gate, e_up, sums, [p], [g], [hid]
    )
    return new_m, held, sums


def shards(tokens, targets, norm_gain, weights, probe_signs, m_state, v_state):
    probes = lax.axis_size("probe")
    chips = lax.axis_size("mp") // 2
    quarter = tokens.shape[1] // probes
    first = lax.axis_index("probe") * quarter
    normed = norm(tokens, norm_gain)
    offset = lax.dynamic_slice_in_dim(tokens, first, quarter, 1).astype(
        F32
    ) - lax.dynamic_slice_in_dim(targets, first, quarter, 1).astype(F32)
    path = near_path if chips == 4 else far_path
    new_m, held, sums = path(normed, offset, weights, probe_signs, m_state, chips, probes)
    sums = [sums] + [to_probe(sums, probes, flip) for flip in range(1, probes)]
    hess, new_v, update = update_step(sums, v_state.transpose(0, 2, 1), held)
    return (hess.transpose(0, 2, 1), new_m, new_v.transpose(0, 2, 1), update)


def solution(mesh):
    return jax.shard_map(
        shards,
        mesh=mesh,
        in_specs=(
            P("mp", None),
            P("mp", None),
            P(),
            P(None, "mp", None),
            P("probe", None, "mp", None),
            P(None, "mp", None),
            P(None, "mp", None),
        ),
        out_specs=(
            P(None, "mp", None),
            P(None, "mp", None),
            P(None, "mp", None),
            P(None, "mp", None),
        ),
        check_vma=False,
    )
```

time: 183 us -> 187 us (1.022)
  local copies, waits for them, and re-layouts: 4.19 us -> 17.8 us
  Pallas kernels: 72.6 us -> 63.5 us
  waiting for transfers between devices: 64.2 us -> 67.9 us
  starting transfers between devices: 36.9 us -> 35 us
    pallas_call x9 -> x11, Pallas kernels: 72.6 us -> 52.1 us  [call(): pl.pallas_call(body, grid=grid, in_specs=in_specs, out_specs=out_specs, o...]
    unnamed x42 -> x82, local copies, waits for them, and re-layouts: 4.1 us -> 17.8 us
    pallas_call x0 -> x2, Pallas kernels: none -> 11.4 us  [load(): pl.pallas_call(lambda *refs: load_kernel(plan, refs), name='load', in_spe...]
    ppermute x6, waiting for transfers between devices: 4.01 us -> 7.16 us  [to_probe(): return lax.ppermute(x, 'probe', [(i, i ^ flip) for i in range(probes)])]
    ppermute x15, starting transfers between devices: 26.9 us -> 24.7 us  [to_chip(): return lax.ppermute(x, 'mp', pairs)]
  transfers between devices with their start and end apart: 36 -> 36, of which waited for: 17 -> 17; matrix products, arithmetic and copies ran while one was open for 2% -> 1% of each run, Pallas kernels for 26% -> 19%
where the time goes in v1:
time: 187 us; the launch traced here: 186 us
  waiting for transfers between devices  67.9 us (36%)
  Pallas kernels  63.5 us (34%)
  starting transfers between devices  35 us (19%)
  local copies, waits for them, and re-layouts  17.8 us (10%)
    ppermute x15, waiting for transfers between devices, to_chip(): return lax.ppermute(x, 'mp', pairs)  58.3 us
    pallas_call x11, Pallas kernels, call(): pl.pallas_call(body, grid=grid, in_specs=in_specs, out_specs=out_specs, o...  52.1 us
    ppermute x15, starting transfers between devices, to_chip(): return lax.ppermute(x, 'mp', pairs)  24.7 us
    unnamed x82, local copies, waits for them, and re-layouts  17.8 us
    pallas_call x2, Pallas kernels, load(): pl.pallas_call(lambda *refs: load_kernel(plan, refs), name='load', in_spe...  11.4 us
    ppermute x6, starting transfers between devices, to_probe(): return lax.ppermute(x, 'probe', [(i, i ^ flip) for i in range(probes)])  8.05 us
    ppermute x6, waiting for transfers between devices, to_probe(): return lax.ppermute(x, 'probe', [(i, i ^ flip) for i in range(probes)])  7.16 us
  transfers between devices with their start and end apart: 36, of which 17 were waited for; matrix products, arithmetic and copies ran while one was open for 1% of the time, Pallas kernels for 19%

profile of v1, /device:TPU:0, one launch (start us, length us, event | category | flops | bytes accessed | tf_op | source)
XLA Modules:
  0.0 186.5 jit_solution(8060011961273001275)
XLA Ops:
  1.7 3.1 %collective-permute-start = (bf16[64,2048]{1,0:T(8,128)(2,1)S(1)}, bf16[64,2048]{1,0:T(8,128)(2,1)S(1)}, u32[]{:S(2)}, u32[]{:S(2)}) collective-permute-start(bf16[64,2048]{1,0:T(8,128)(2,1)S(1)} %shard_map.102.refs_0_), channel_id=1, source_target_pairs={{0,2},{1,3},{2,0},{3,1},{4,6},{5,7},{6,4},{7,5},{8,10},{9,11},{10,... | collective-permute-start | bytes 786440 | tf_op jit(solution)/shard_map/ppermute | solution.py:589
  4.9 2.5 %collective-permute-start.4 = (bf16[64,2048]{1,0:T(8,128)(2,1)S(1)}, bf16[64,2048]{1,0:T(8,128)(2,1)S(1)}, u32[]{:S(2)}, u32[]{:S(2)}) collective-permute-start(bf16[64,2048]{1,0:T(8,128)(2,1)S(1)} %shard_map.102.refs_0_), channel_id=1, source_target_pairs={{0,6},{1,7},{2,4},{3,5},{4,2},{5,3},{6,0},{7,1},{8,14},{9,15},{10,... | collective-permute-start | bytes 786440 | tf_op jit(solution)/shard_map/ppermute | solution.py:589
  7.5 4.1 %collective-permute-done.refs_1_ = bf16[64,2048]{1,0:T(8,128)(2,1)S(1)} collective-permute-done((bf16[64,2048]{1,0:T(8,128)(2,1)S(1)}, bf16[64,2048]{1,0:T(8,128)(2,1)S(1)}, u32[]{:S(2)}, u32[]{:S(2)}) %collective-permute-start) | collective-permute-done | bytes 262176 | tf_op jit(solution)/shard_map/ppermute | solution.py:589
  11.6 8.6 %collective-permute-done.4.refs_1_ = bf16[64,2048]{1,0:T(8,128)(2,1)S(1)} collective-permute-done((bf16[64,2048]{1,0:T(8,128)(2,1)S(1)}, bf16[64,2048]{1,0:T(8,128)(2,1)S(1)}, u32[]{:S(2)}, u32[]{:S(2)}) %collective-permute-start.4) | collective-permute-done | bytes 262176 | tf_op jit(solution)/shard_map/ppermute | solution.py:589
  20.2 10.1 %collective-permute-done.3.refs_0_ = bf16[64,2048]{1,0:T(8,128)(2,1)S(1)} collective-permute-done((bf16[64,2048]{1,0:T(8,128)(2,1)S(1)}, bf16[64,2048]{1,0:T(8,128)(2,1)S(1)}, u32[]{:S(2)}, u32[]{:S(2)}) %collective-permute-start.3) | collective-permute-done | bytes 262176 | tf_op jit(solution)/shard_map/ppermute | solution.py:589
  30.3 5.7 %load.2 = (bf16[6,320,2048]{2,1,0:T(8,128)(2,1)S(1)}, bf16[6,320,2048]{2,1,0:T(8,128)(2,1)S(1)}) custom-call(bf16[6,320,2048]{2,1,0:T(8,128)(2,1)} %bitcast.16, bf16[6,320,2048]{2,1,0:T(8,128)(2,1)} %bitcast.17), custom_call_target="tpu_custom_call" | custom-call | flops 503316480 | bytes 62914560 | tf_op jit(solution)/shard_map/load/pallas_call | solution.py:336
  36.1 3.5 %shard_map.103 = (bf16[512,2048]{1,0:T(8,128)(2,1)S(1)}, f32[640,256]{1,0:T(8,128)S(1)}, f32[640,256]{1,0:T(8,128)S(1)}, f32[640,256]{1,0:T(8,128)S(1)}, f32[640...) custom-call(bf16[64,2048]{1,0:T(8,128)(2,1)S(1)} %shard_map.102.refs_0_, ...), custom_call_target="tpu_custom_call" | custom-call | flops 1342177280 | bytes 12910592 | tf_op jit(solution)/shard_map/pallas_call | solution.py:86
  39.6 1.8 shard_map.104
  43.1 3.5 %shard_map.105 = (bf16[512,2048]{1,0:T(8,128)(2,1)S(1)}, f32[640,256]{1,0:T(8,128)S(1)}, f32[640,256]{1,0:T(8,128)S(1)}, f32[640,256]{1,0:T(8,128)S(1)}, f32[640...) custom-call(bf16[64,2048]{1,0:T(8,128)(2,1)S(1)} %collective-permute, ...), custom_call_target="tpu_custom_call", output_to_operand_aliasing={{0}: (5, {})} | custom-call | flops 1342177280 | bytes 12910592 | tf_op jit(solution)/shard_map/pallas_call | solution.py:86
  46.6 1.8 shard_map.106
  48.5 4.8 %shard_map.107 = (f32[256,2048]{1,0:T(8,128)S(1)}, bf16[256,2048]{1,0:T(8,128)(2,1)}) custom-call(bf16[3,640,2048]{2,1,0:T(8,128)(2,1)S(1)} %bitcast.11, bf16[3,640,2048]{2,1,0:T(8,128)(2,1)S(1)} %bitcast.14, bf16[640,256]{1,0:T(8,128)(2,1)S(1)} %get-tuple-element.53.refs_2_.refs_22_, bf16[640,256]{1,0:T(8,128)(2,1)S(1)} %get-tuple-element.59.refs_3_.refs_23_, ...), custom_call_target="tpu_custom_call" | custom-call | flops 2684354560 | bytes 8388608 | tf_op jit(solution)/shard_map/pallas_call | solution.py:86
  55.7 2.2 %collective-permute-done.18.refs_2_ = bf16[128,512]{1,0:T(8,128)(2,1)S(1)} collective-permute-done((bf16[128,512]{1,0:T(8,128)(2,1)S(1)}, bf16[128,512]{1,0:T(8,128)(2,1)S(1)}, u32[]{:S(2)}, u32[]{:S(2)}) %collective-permute-start.18) | collective-permute-done | bytes 131104 | tf_op jit(solution)/shard_map/ppermute | solution.py:584
  58.7 3.2 %collective-permute-start.21 = (bf16[64,512]{1,0:T(8,128)(2,1)}, bf16[64,512]{1,0:T(8,128)(2,1)}, u32[]{:S(2)}, u32[]{:S(2)}) collective-permute-start(bf16[64,512]{1,0:T(8,128)(2,1)} %get-tuple-element.74), channel_id=1, source_target_pairs={{0,4},{1,5},{2,6},{3,7},{4,0},{5,1},{6,2},{7,3},{8,12},{9,13},{10,... | collective-permute-start | bytes 196616 | tf_op jit(solution)/shard_map/ppermute | solution.py:589
  64.5 1.9 %collective-permute-done.21 = bf16[64,512]{1,0:T(8,128)(2,1)} collective-permute-done((bf16[64,512]{1,0:T(8,128)(2,1)}, bf16[64,512]{1,0:T(8,128)(2,1)}, u32[]{:S(2)}, u32[]{:S(2)}) %collective-permute-start.21) | collective-permute-done | bytes 65568 | tf_op jit(solution)/shard_map/ppermute | solution.py:589
  66.4 2.0 %collective-permute-done.22 = bf16[64,512]{1,0:T(8,128)(2,1)} collective-permute-done((bf16[64,512]{1,0:T(8,128)(2,1)}, bf16[64,512]{1,0:T(8,128)(2,1)}, u32[]{:S(2)}, u32[]{:S(2)}) %collective-permute-start.22) | collective-permute-done | bytes 65568 | tf_op jit(solution)/shard_map/ppermute | solution.py:589
  69.3 2.1 %collective-permute-start.25 = (bf16[64,512]{1,0:T(8,128)(2,1)S(1)}, bf16[64,512]{1,0:T(8,128)(2,1)S(1)}, u32[]{:S(2)}, u32[]{:S(2)}) collective-permute-start(bf16[64,512]{1,0:T(8,128)(2,1)S(1)} %multiply_convert_fusion.1), channel_id=1, source_target_pairs={{0,6},{1,7},{2,4},{3,5},{4,2},{5,3},{6,0},{7,1},{8,14},{9,15},{10,... | collective-permute-start | bytes 196616 | tf_op jit(solution)/shard_map/ppermute | solution.py:589
  71.9 1.9 %collective-permute-start.23 = (bf16[64,512]{1,0:T(8,128)(2,1)S(1)}, bf16[64,512]{1,0:T(8,128)(2,1)S(1)}, u32[]{:S(2)}, u32[]{:S(2)}) collective-permute-start(bf16[64,512]{1,0:T(8,128)(2,1)S(1)} %multiply_convert_fusion.1), channel_id=1, source_target_pairs={{0,2},{1,3},{2,0},{3,1},{4,6},{5,7},{6,4},{7,5},{8,10},{9,11},{10,... | collective-permute-start | bytes 196616 | tf_op jit(solution)/shard_map/ppermute | solution.py:589
  73.8 2.4 %collective-permute-done.25 = bf16[64,512]{1,0:T(8,128)(2,1)S(1)} collective-permute-done((bf16[64,512]{1,0:T(8,128)(2,1)S(1)}, bf16[64,512]{1,0:T(8,128)(2,1)S(1)}, u32[]{:S(2)}, u32[]{:S(2)}) %collective-permute-start.25) | collective-permute-done | bytes 65568 | tf_op jit(solution)/shard_map/ppermute | solution.py:589
  77.9 2.5 %collective-permute-start.28 = (bf16[256,512]{1,0:T(8,128)(2,1)S(1)}, bf16[256,512]{1,0:T(8,128)(2,1)S(1)}, u32[]{:S(2)}, u32[]{:S(2)}) collective-permute-start(bf16[256,512]{1,0:T(8,128)(2,1)S(1)} %pad_maximum_fusion.refs_0_), channel_id=1, source_target_pairs={{0,24},{8,16},{16,8},{24,0},{1,25},{9,17},{17,9},{25,1},{2,26},{10... | collective-permute-start | bytes 786440 | tf_op jit(solution)/shard_map/ppermute | solution.py:593
  84.2 2.5 %collective-permute-start.9 = (bf16[64,2048]{1,0:T(8,128)(2,1)S(1)}, bf16[64,2048]{1,0:T(8,128)(2,1)S(1)}, u32[]{:S(2)}, u32[]{:S(2)}) collective-permute-start(bf16[64,2048]{1,0:T(8,128)(2,1)S(1)} %get-tuple-element.66), channel_id=1, source_target_pairs={{0,4},{1,5},{2,6},{3,7},{4,0},{5,1},{6,2},{7,3},{8,12},{9,13},{10,... | collective-permute-start | bytes 786440 | tf_op jit(solution)/shard_map/ppermute | solution.py:589
  88.4 3.9 %collective-permute-done.27.refs_2_ = bf16[256,512]{1,0:T(8,128)(2,1)S(1)} collective-permute-done((bf16[256,512]{1,0:T(8,128)(2,1)S(1)}, bf16[256,512]{1,0:T(8,128)(2,1)S(1)}, u32[]{:S(2)}, u32[]{:S(2)}) %collective-permute-start.27) | collective-permute-done | bytes 262176 | tf_op jit(solution)/shard_map/ppermute | solution.py:593
  93.8 2.3 %collective-permute-done.8 = bf16[64,2048]{1,0:T(8,128)(2,1)S(1)} collective-permute-done((bf16[64,2048]{1,0:T(8,128)(2,1)S(1)}, bf16[64,2048]{1,0:T(8,128)(2,1)S(1)}, u32[]{:S(2)}, u32[]{:S(2)}) %collective-permute-start.8) | collective-permute-done | bytes 262176 | tf_op jit(solution)/shard_map/ppermute | solution.py:589
  96.0 9.4 %collective-permute-done.9 = bf16[64,2048]{1,0:T(8,128)(2,1)S(1)} collective-permute-done((bf16[64,2048]{1,0:T(8,128)(2,1)S(1)}, bf16[64,2048]{1,0:T(8,128)(2,1)S(1)}, u32[]{:S(2)}, u32[]{:S(2)}) %collective-permute-start.9) | collective-permute-done | bytes 262176 | tf_op jit(solution)/shard_map/ppermute | solution.py:589
  105.6 2.1 %collective-permute-start.15 = (bf16[64,2048]{1,0:T(8,128)(2,1)S(1)}, bf16[64,2048]{1,0:T(8,128)(2,1)S(1)}, u32[]{:S(2)}, u32[]{:S(2)}) collective-permute-start(bf16[64,2048]{1,0:T(8,128)(2,1)S(1)} %multiply_convert_fusion.refs_0_), channel_id=1, source_target_pairs={{0,6},{1,7},{2,4},{3,5},{4,2},{5,3},{6,0},{7,1},{8,14},{9,15},{10,... | collective-permute-start | bytes 786440 | tf_op jit(solution)/shard_map/ppermute | solution.py:589
  107.7 3.6 %collective-permute-start.14 = (bf16[64,2048]{1,0:T(8,128)(2,1)S(1)}, bf16[64,2048]{1,0:T(8,128)(2,1)S(1)}, u32[]{:S(2)}, u32[]{:S(2)}) collective-permute-start(bf16[64,2048]{1,0:T(8,128)(2,1)S(1)} %multiply_convert_fusion.refs_0_), channel_id=1, source_target_pairs={{0,4},{1,5},{2,6},{3,7},{4,0},{5,1},{6,2},{7,3},{8,12},{9,13},{10,... | collective-permute-start | bytes 786440 | tf_op jit(solution)/shard_map/ppermute | solution.py:589
  111.5 5.8 %load.3.refs_10_ = f32[12,160,2048]{2,1,0:T(8,128)S(1)} custom-call(f32[12,160,2048]{2,1,0:T(8,128)} %bitcast.18), custom_call_target="tpu_custom_call" | custom-call | flops 251658240 | bytes 31457280 | tf_op jit(solution)/shard_map/load/pallas_call | solution.py:336
  118.0 14.5 %collective-permute-done.14.refs_4_ = bf16[64,2048]{1,0:T(8,128)(2,1)S(1)} collective-permute-done((bf16[64,2048]{1,0:T(8,128)(2,1)S(1)}, bf16[64,2048]{1,0:T(8,128)(2,1)S(1)}, u32[]{:S(2)}, u32[]{:S(2)}) %collective-permute-start.14) | collective-permute-done | bytes 262176 | tf_op jit(solution)/shard_map/ppermute | solution.py:589
  133.7 15.9 %shard_map.110 = (f32[3,640,2048]{2,1,0:T(8,128)}, f32[12,160,2048]{2,1,0:T(8,128)S(1)}, f32[640,512]{1,0:T(8,128)S(1)}, f32[640,512]{1,0:T(8,128)S(1)}, f32[640,128]{1,0:T(8,128)S(1)}) custom-call(bf16[256,512]{1,0:T(8,128)(2,1)} %copy-done.33, bf16[256,512]{1,0:T(8,128)(2,1)} %copy-done.37, ...), custom_call_target="tpu_custom_call", output_to_operand_aliasing={{1}: (10, {})} | custom-call | flops 8053063680 | bytes 45875200 | tf_op jit(solution)/shard_map/pallas_call | solution.py:86
  149.7 5.8 %copy-done = f32[12,160,2048]{2,1,0:T(8,128)} copy-done((f32[12,160,2048]{2,1,0:T(8,128)}, f32[12,160,2048]{2,1,0:T(8,128)S(1)}, u32[]{:S(2)}) %copy-start) | copy-done | bytes 15728664
  162.1 9.6 %shard_map.111.a = f32[48,320]{1,0:T(8,128)S(1)} custom-call(bf16[64,2048]{1,0:T(8,128)(2,1)S(1)} %multiply_convert_fusion.refs_0_, bf16[64,2048]{1,0:T(8,128)(2,1)S(1)} %collective-permute-done.11.refs_1_, bf16[64,2048]{1,0:T(8,128)(2,1)S(1)} %copy-done.25, bf16[64,2048]{1,0:T(8,128)(2,1)S(1)} %copy-done.31, ...), custom_call_target="tpu_custom_call" | custom-call | flops 5368709120 | bytes 16384000 | tf_op jit(solution)/shard_map/pallas_call | solution.py:86
  175.3 2.0 %collective-permute-done.35.d = f32[48,320]{1,0:T(8,128)S(1)} collective-permute-done((f32[48,320]{1,0:T(8,128)S(1)}, f32[48,320]{1,0:T(8,128)S(1)}, u32[]{:S(2)}, u32[]{:S(2)}) %collective-permute-start.35) | collective-permute-done | bytes 61472 | tf_op jit(solution)/shard_map/ppermute | solution.py:593
  178.5 8.0 %shard_map.112 = (f32[3,16,320]{2,1,0:T(8,128)}, f32[3,16,320]{2,1,0:T(8,128)}, f32[3,640,2048]{2,1,0:T(8,128)}) custom-call(f32[48,320]{1,0:T(8,128)S(1)} %shard_map.111.a, f32[48,320]{1,0:T(8,128)S(1)} %collective-permute-done.33.b, f32[48,320]{1,0:T(8,128)S(1)} %collective-permute-done.34.c, f32[48,320]{1,0:T(8,128)S(1)} %collective-permute-done.35.d, ...), custom_call_target="tpu_custom_call" | custom-call | flops 7864320 | bytes 31457280 | tf_op jit(solution)/shard_map/pallas_call | solution.py:86
  (138 shorter events, 32.4 us)
Async XLA Ops:
  1.7 9.8 %collective-permute-start = (bf16[64,2048]{1,0:T(8,128)(2,1)S(1)}, bf16[64,2048]{1,0:T(8,128)(2,1)S(1)}, u32[]{:S(2)}, u32[]{:S(2)}) collective-permute-start(bf16[64,2048]{1,0:T(8,128)(2,1)S(1)} %shard_map.102.refs_0_), channel_id=1, source_target_pairs={{0,2},{1,3},{2,0},{3,1},{4,6},{5,7},{6,4},{7,5},{8,10},{9,11},{10,... | collective-permute-start | bytes 786440 | tf_op jit(solution)/shard_map/ppermute | solution.py:589
  4.9 15.3 %collective-permute-start.4 = (bf16[64,2048]{1,0:T(8,128)(2,1)S(1)}, bf16[64,2048]{1,0:T(8,128)(2,1)S(1)}, u32[]{:S(2)}, u32[]{:S(2)}) collective-permute-start(bf16[64,2048]{1,0:T(8,128)(2,1)S(1)} %shard_map.102.refs_0_), channel_id=1, source_target_pairs={{0,6},{1,7},{2,4},{3,5},{4,2},{5,3},{6,0},{7,1},{8,14},{9,15},{10,... | collective-permute-start | bytes 786440 | tf_op jit(solution)/shard_map/ppermute | solution.py:589
  7.3 23.0 %collective-permute-start.3 = (bf16[64,2048]{1,0:T(8,128)(2,1)S(1)}, bf16[64,2048]{1,0:T(8,128)(2,1)S(1)}, u32[]{:S(2)}, u32[]{:S(2)}) collective-permute-start(bf16[64,2048]{1,0:T(8,128)(2,1)S(1)} %shard_map.102.refs_0_), channel_id=1, source_target_pairs={{0,4},{1,5},{2,6},{3,7},{4,0},{5,1},{6,2},{7,3},{8,12},{9,13},{10,... | collective-permute-start | bytes 786440 | tf_op jit(solution)/shard_map/ppermute | solution.py:589
  7.5 28.6 %collective-permute-start.1 = (bf16[64,2048]{1,0:T(8,128)(2,1)S(1)}, bf16[64,2048]{1,0:T(8,128)(2,1)S(1)}, u32[]{:S(2)}, u32[]{:S(2)}) collective-permute-start(bf16[64,2048]{1,0:T(8,128)(2,1)S(1)} %shard_map.102.refs_0_), channel_id=1, source_target_pairs={{0,1},{1,0},{2,3},{3,2},{4,5},{5,4},{6,7},{7,6},{8,9},{9,8},{10,11... | collective-permute-start | bytes 786440 | tf_op jit(solution)/shard_map/ppermute | solution.py:584
  11.6 24.5 %collective-permute-start.2 = (bf16[64,2048]{1,0:T(8,128)(2,1)S(1)}, bf16[64,2048]{1,0:T(8,128)(2,1)S(1)}, u32[]{:S(2)}, u32[]{:S(2)}) collective-permute-start(bf16[64,2048]{1,0:T(8,128)(2,1)S(1)} %collective-permute-done.refs_1_), channel_id=1, source_target_pairs={{0,1},{1,0},{2,3},{3,2},{4,5},{5,4},{6,7},{7,6},{8,9},{9,8},{10,11... | collective-permute-start | bytes 786440 | tf_op jit(solution)/shard_map/ppermute | solution.py:584
  20.2 22.9 %collective-permute-start.6 = (bf16[64,2048]{1,0:T(8,128)(2,1)S(1)}, bf16[64,2048]{1,0:T(8,128)(2,1)S(1)}, u32[]{:S(2)}, u32[]{:S(2)}) collective-permute-start(bf16[64,2048]{1,0:T(8,128)(2,1)S(1)} %collective-permute-done.4.refs_1_), channel_id=1, source_target_pairs={{0,1},{1,0},{2,3},{3,2},{4,5},{5,4},{6,7},{7,6},{8,9},{9,8},{10,11... | collective-permute-start | bytes 786440 | tf_op jit(solution)/shard_map/ppermute | solution.py:584
  30.3 12.8 %collective-permute-start.5 = (bf16[64,2048]{1,0:T(8,128)(2,1)S(1)}, bf16[64,2048]{1,0:T(8,128)(2,1)S(1)}, u32[]{:S(2)}, u32[]{:S(2)}) collective-permute-start(bf16[64,2048]{1,0:T(8,128)(2,1)S(1)} %collective-permute-done.3.refs_0_), channel_id=1, source_target_pairs={{0,1},{1,0},{2,3},{3,2},{4,5},{5,4},{6,7},{7,6},{8,9},{9,8},{10,11... | collective-permute-start | bytes 786440 | tf_op jit(solution)/shard_map/ppermute | solution.py:584
  54.6 26.3 %collective-permute-start.7 = (bf16[256,2048]{1,0:T(8,128)(2,1)}, bf16[256,2048]{1,0:T(8,128)(2,1)}, u32[]{:S(2)}, u32[]{:S(2)}) collective-permute-start(bf16[256,2048]{1,0:T(8,128)(2,1)} %get-tuple-element.63), channel_id=1, source_target_pairs={{0,1},{1,0},{2,3},{3,2},{4,5},{5,4},{6,7},{7,6},{8,9},{9,8},{10,11... | collective-permute-start | bytes 3145736 | tf_op jit(solution)/shard_map/ppermute | solution.py:584
  58.7 5.8 %collective-permute-start.20 = (bf16[64,512]{1,0:T(8,128)(2,1)}, bf16[64,512]{1,0:T(8,128)(2,1)}, u32[]{:S(2)}, u32[]{:S(2)}) collective-permute-start(bf16[64,512]{1,0:T(8,128)(2,1)} %get-tuple-element.73), channel_id=1, source_target_pairs={{0,2},{1,3},{2,0},{3,1},{4,6},{5,7},{6,4},{7,5},{8,10},{9,11},{10,... | collective-permute-start | bytes 196616 | tf_op jit(solution)/shard_map/ppermute | solution.py:589
  58.7 7.6 %collective-permute-start.21 = (bf16[64,512]{1,0:T(8,128)(2,1)}, bf16[64,512]{1,0:T(8,128)(2,1)}, u32[]{:S(2)}, u32[]{:S(2)}) collective-permute-start(bf16[64,512]{1,0:T(8,128)(2,1)} %get-tuple-element.74), channel_id=1, source_target_pairs={{0,4},{1,5},{2,6},{3,7},{4,0},{5,1},{6,2},{7,3},{8,12},{9,13},{10,... | collective-permute-start | bytes 196616 | tf_op jit(solution)/shard_map/ppermute | solution.py:589
  61.9 6.4 %collective-permute-start.22 = (bf16[64,512]{1,0:T(8,128)(2,1)}, bf16[64,512]{1,0:T(8,128)(2,1)}, u32[]{:S(2)}, u32[]{:S(2)}) collective-permute-start(bf16[64,512]{1,0:T(8,128)(2,1)} %get-tuple-element.75), channel_id=1, source_target_pairs={{0,6},{1,7},{2,4},{3,5},{4,2},{5,3},{6,0},{7,1},{8,14},{9,15},{10,... | collective-permute-start | bytes 196616 | tf_op jit(solution)/shard_map/ppermute | solution.py:589
  69.3 6.8 %collective-permute-start.25 = (bf16[64,512]{1,0:T(8,128)(2,1)S(1)}, bf16[64,512]{1,0:T(8,128)(2,1)S(1)}, u32[]{:S(2)}, u32[]{:S(2)}) collective-permute-start(bf16[64,512]{1,0:T(8,128)(2,1)S(1)} %multiply_convert_fusion.1), channel_id=1, source_target_pairs={{0,6},{1,7},{2,4},{3,5},{4,2},{5,3},{6,0},{7,1},{8,14},{9,15},{10,... | collective-permute-start | bytes 196616 | tf_op jit(solution)/shard_map/ppermute | solution.py:589
  71.4 6.4 %collective-permute-start.24 = (bf16[64,512]{1,0:T(8,128)(2,1)S(1)}, bf16[64,512]{1,0:T(8,128)(2,1)S(1)}, u32[]{:S(2)}, u32[]{:S(2)}) collective-permute-start(bf16[64,512]{1,0:T(8,128)(2,1)S(1)} %multiply_convert_fusion.1), channel_id=1, source_target_pairs={{0,4},{1,5},{2,6},{3,7},{4,0},{5,1},{6,2},{7,3},{8,12},{9,13},{10,... | collective-permute-start | bytes 196616 | tf_op jit(solution)/shard_map/ppermute | solution.py:589
  71.9 5.9 %collective-permute-start.23 = (bf16[64,512]{1,0:T(8,128)(2,1)S(1)}, bf16[64,512]{1,0:T(8,128)(2,1)S(1)}, u32[]{:S(2)}, u32[]{:S(2)}) collective-permute-start(bf16[64,512]{1,0:T(8,128)(2,1)S(1)} %multiply_convert_fusion.1), channel_id=1, source_target_pairs={{0,2},{1,3},{2,0},{3,1},{4,6},{5,7},{6,4},{7,5},{8,10},{9,11},{10,... | collective-permute-start | bytes 196616 | tf_op jit(solution)/shard_map/ppermute | solution.py:589
  77.9 10.5 %collective-permute-start.28 = (bf16[256,512]{1,0:T(8,128)(2,1)S(1)}, bf16[256,512]{1,0:T(8,128)(2,1)S(1)}, u32[]{:S(2)}, u32[]{:S(2)}) collective-permute-start(bf16[256,512]{1,0:T(8,128)(2,1)S(1)} %pad_maximum_fusion.refs_0_), channel_id=1, source_target_pairs={{0,24},{8,16},{16,8},{24,0},{1,25},{9,17},{17,9},{25,1},{2,26},{10... | collective-permute-start | bytes 786440 | tf_op jit(solution)/shard_map/ppermute | solution.py:593
  80.4 11.9 %collective-permute-start.27 = (bf16[256,512]{1,0:T(8,128)(2,1)S(1)}, bf16[256,512]{1,0:T(8,128)(2,1)S(1)}, u32[]{:S(2)}, u32[]{:S(2)}) collective-permute-start(bf16[256,512]{1,0:T(8,128)(2,1)S(1)} %pad_maximum_fusion.refs_0_), channel_id=1, source_target_pairs={{0,16},{8,24},{16,0},{24,8},{1,17},{9,25},{17,1},{25,9},{2,18},{10... | collective-permute-start | bytes 786440 | tf_op jit(solution)/shard_map/ppermute | solution.py:593
  83.9 12.1 %collective-permute-start.8 = (bf16[64,2048]{1,0:T(8,128)(2,1)S(1)}, bf16[64,2048]{1,0:T(8,128)(2,1)S(1)}, u32[]{:S(2)}, u32[]{:S(2)}) collective-permute-start(bf16[64,2048]{1,0:T(8,128)(2,1)S(1)} %get-tuple-element.65), channel_id=1, source_target_pairs={{0,2},{1,3},{2,0},{3,1},{4,6},{5,7},{6,4},{7,5},{8,10},{9,11},{10,... | collective-permute-start | bytes 786440 | tf_op jit(solution)/shard_map/ppermute | solution.py:589
  84.2 21.3 %collective-permute-start.9 = (bf16[64,2048]{1,0:T(8,128)(2,1)S(1)}, bf16[64,2048]{1,0:T(8,128)(2,1)S(1)}, u32[]{:S(2)}, u32[]{:S(2)}) collective-permute-start(bf16[64,2048]{1,0:T(8,128)(2,1)S(1)} %get-tuple-element.66), channel_id=1, source_target_pairs={{0,4},{1,5},{2,6},{3,7},{4,0},{5,1},{6,2},{7,3},{8,12},{9,13},{10,... | collective-permute-start | bytes 786440 | tf_op jit(solution)/shard_map/ppermute | solution.py:589
  86.6 18.8 %collective-permute-start.10 = (bf16[64,2048]{1,0:T(8,128)(2,1)S(1)}, bf16[64,2048]{1,0:T(8,128)(2,1)S(1)}, u32[]{:S(2)}, u32[]{:S(2)}) collective-permute-start(bf16[64,2048]{1,0:T(8,128)(2,1)S(1)} %get-tuple-element.67), channel_id=1, source_target_pairs={{0,6},{1,7},{2,4},{3,5},{4,2},{5,3},{6,0},{7,1},{8,14},{9,15},{10,... | collective-permute-start | bytes 786440 | tf_op jit(solution)/shard_map/ppermute | solution.py:589
  88.3 19.4 %collective-permute-start.29 = (bf16[256,512]{1,0:T(8,128)(2,1)S(1)}, bf16[256,512]{1,0:T(8,128)(2,1)S(1)}, u32[]{:S(2)}, u32[]{:S(2)}) collective-permute-start(bf16[256,512]{1,0:T(8,128)(2,1)S(1)} %pad_maximum_fusion.refs_0_), channel_id=1, source_target_pairs={{0,1},{1,0},{2,3},{3,2},{4,5},{5,4},{6,7},{7,6},{8,9},{9,8},{10,11... | collective-permute-start | bytes 786440 | tf_op jit(solution)/shard_map/ppermute | solution.py:584
  92.3 19.0 %collective-permute-start.26 = (bf16[256,512]{1,0:T(8,128)(2,1)S(1)}, bf16[256,512]{1,0:T(8,128)(2,1)S(1)}, u32[]{:S(2)}, u32[]{:S(2)}) collective-permute-start(bf16[256,512]{1,0:T(8,128)(2,1)S(1)} %pad_maximum_fusion.refs_0_), channel_id=1, source_target_pairs={{0,8},{8,0},{16,24},{24,16},{1,9},{9,1},{17,25},{25,17},{2,10},{10... | collective-permute-start | bytes 786440 | tf_op jit(solution)/shard_map/ppermute | solution.py:593
  96.0 15.3 %collective-permute-start.32 = (bf16[256,512]{1,0:T(8,128)(2,1)S(1)}, bf16[256,512]{1,0:T(8,128)(2,1)S(1)}, u32[]{:S(2)}, u32[]{:S(2)}) collective-permute-start(bf16[256,512]{1,0:T(8,128)(2,1)S(1)} %collective-permute-done.28.refs_3_), channel_id=1, source_target_pairs={{0,1},{1,0},{2,3},{3,2},{4,5},{5,4},{6,7},{7,6},{8,9},{9,8},{10,11... | collective-permute-start | bytes 786440 | tf_op jit(solution)/shard_map/ppermute | solution.py:584
  105.5 11.9 %collective-permute-start.31 = (bf16[256,512]{1,0:T(8,128)(2,1)S(1)}, bf16[256,512]{1,0:T(8,128)(2,1)S(1)}, u32[]{:S(2)}, u32[]{:S(2)}) collective-permute-start(bf16[256,512]{1,0:T(8,128)(2,1)S(1)} %collective-permute-done.27.refs_2_), channel_id=1, source_target_pairs={{0,1},{1,0},{2,3},{3,2},{4,5},{5,4},{6,7},{7,6},{8,9},{9,8},{10,11... | collective-permute-start | bytes 786440 | tf_op jit(solution)/shard_map/ppermute | solution.py:584
  105.6 12.3 %collective-permute-start.15 = (bf16[64,2048]{1,0:T(8,128)(2,1)S(1)}, bf16[64,2048]{1,0:T(8,128)(2,1)S(1)}, u32[]{:S(2)}, u32[]{:S(2)}) collective-permute-start(bf16[64,2048]{1,0:T(8,128)(2,1)S(1)} %multiply_convert_fusion.refs_0_), channel_id=1, source_target_pairs={{0,6},{1,7},{2,4},{3,5},{4,2},{5,3},{6,0},{7,1},{8,14},{9,15},{10,... | collective-permute-start | bytes 786440 | tf_op jit(solution)/shard_map/ppermute | solution.py:589
  107.7 24.7 %collective-permute-start.14 = (bf16[64,2048]{1,0:T(8,128)(2,1)S(1)}, bf16[64,2048]{1,0:T(8,128)(2,1)S(1)}, u32[]{:S(2)}, u32[]{:S(2)}) collective-permute-start(bf16[64,2048]{1,0:T(8,128)(2,1)S(1)} %multiply_convert_fusion.refs_0_), channel_id=1, source_target_pairs={{0,4},{1,5},{2,6},{3,7},{4,0},{5,1},{6,2},{7,3},{8,12},{9,13},{10,... | collective-permute-start | bytes 786440 | tf_op jit(solution)/shard_map/ppermute | solution.py:589
  111.3 21.1 %collective-permute-start.11 = (bf16[64,2048]{1,0:T(8,128)(2,1)S(1)}, bf16[64,2048]{1,0:T(8,128)(2,1)S(1)}, u32[]{:S(2)}, u32[]{:S(2)}) collective-permute-start(bf16[64,2048]{1,0:T(8,128)(2,1)S(1)} %multiply_convert_fusion.refs_0_), channel_id=1, source_target_pairs={{0,2},{1,3},{2,0},{3,1},{4,6},{5,7},{6,4},{7,5},{8,10},{9,11},{10,... | collective-permute-start | bytes 786440 | tf_op jit(solution)/shard_map/ppermute | solution.py:589
  111.3 21.6 %collective-permute-start.30 = (bf16[256,512]{1,0:T(8,128)(2,1)S(1)}, bf16[256,512]{1,0:T(8,128)(2,1)S(1)}, u32[]{:S(2)}, u32[]{:S(2)}) collective-permute-start(bf16[256,512]{1,0:T(8,128)(2,1)S(1)} %collective-permute-done.26.refs_1_), channel_id=1, source_target_pairs={{0,1},{1,0},{2,3},{3,2},{4,5},{5,4},{6,7},{7,6},{8,9},{9,8},{10,11... | collective-permute-start | bytes 786440 | tf_op jit(solution)/shard_map/ppermute | solution.py:584
  117.4 38.1 %collective-permute-start.12 = (bf16[64,2048]{1,0:T(8,128)(2,1)S(1)}, bf16[64,2048]{1,0:T(8,128)(2,1)S(1)}, u32[]{:S(2)}, u32[]{:S(2)}) collective-permute-start(bf16[64,2048]{1,0:T(8,128)(2,1)S(1)} %multiply_convert_fusion.refs_0_), channel_id=1, source_target_pairs={{0,1},{1,0},{2,3},{3,2},{4,5},{5,4},{6,7},{7,6},{8,9},{9,8},{10,11... | collective-permute-start | bytes 786440 | tf_op jit(solution)/shard_map/ppermute | solution.py:584
  117.9 38.3 %collective-permute-start.17 = (bf16[64,2048]{1,0:T(8,128)(2,1)S(1)}, bf16[64,2048]{1,0:T(8,128)(2,1)S(1)}, u32[]{:S(2)}, u32[]{:S(2)}) collective-permute-start(bf16[64,2048]{1,0:T(8,128)(2,1)S(1)} %collective-permute-done.15.refs_5_), channel_id=1, source_target_pairs={{0,1},{1,0},{2,3},{3,2},{4,5},{5,4},{6,7},{7,6},{8,9},{9,8},{10,11... | collective-permute-start | bytes 786440 | tf_op jit(solution)/shard_map/ppermute | solution.py:584
  132.5 24.5 %collective-permute-start.16 = (bf16[64,2048]{1,0:T(8,128)(2,1)S(1)}, bf16[64,2048]{1,0:T(8,128)(2,1)S(1)}, u32[]{:S(2)}, u32[]{:S(2)}) collective-permute-start(bf16[64,2048]{1,0:T(8,128)(2,1)S(1)} %collective-permute-done.14.refs_4_), channel_id=1, source_target_pairs={{0,1},{1,0},{2,3},{3,2},{4,5},{5,4},{6,7},{7,6},{8,9},{9,8},{10,11... | collective-permute-start | bytes 786440 | tf_op jit(solution)/shard_map/ppermute | solution.py:584
  132.5 25.2 %collective-permute-start.13 = (bf16[64,2048]{1,0:T(8,128)(2,1)S(1)}, bf16[64,2048]{1,0:T(8,128)(2,1)S(1)}, u32[]{:S(2)}, u32[]{:S(2)}) collective-permute-start(bf16[64,2048]{1,0:T(8,128)(2,1)S(1)} %collective-permute-done.11.refs_1_), channel_id=1, source_target_pairs={{0,1},{1,0},{2,3},{3,2},{4,5},{5,4},{6,7},{7,6},{8,9},{9,8},{10,11... | collective-permute-start | bytes 786440 | tf_op jit(solution)/shard_map/ppermute | solution.py:584
  171.7 5.6 %collective-permute-start.35 = (f32[48,320]{1,0:T(8,128)S(1)}, f32[48,320]{1,0:T(8,128)S(1)}, u32[]{:S(2)}, u32[]{:S(2)}) collective-permute-start(f32[48,320]{1,0:T(8,128)S(1)} %shard_map.111.a), channel_id=1, source_target_pairs={{0,24},{8,16},{16,8},{24,0},{1,25},{9,17},{17,9},{25,1},{2,26},{10... | collective-permute-start | bytes 184328 | tf_op jit(solution)/shard_map/ppermute | solution.py:593
  (45 other events, 467.8 us)

commit v2 on v1

--- a/solution.py
+++ b/solution.py
@@ -56,10 +56,10 @@
 BASE_UNITS = 160
 TANGENT_UNITS = 320
 UPDATE_UNITS = 320
-FORWARD_LIMIT = 24
-BASE_LIMIT = 28
-TANGENT_LIMIT = 32
-UPDATE_LIMIT = 16
+FORWARD_LIMIT = 14
+BASE_LIMIT = 25
+TANGENT_LIMIT = 27
+UPDATE_LIMIT = 9
 
 
 def unit_block(units, wanted):
@@ -297,7 +297,7 @@
             at += 1
 
 
-def fold(owns, gots, rows):
+def fold(owns, gots, rows, keep):
     parts = len(owns)
     blocks = sum(own.shape[0] for own in owns) // rows
     width = owns[0].shape[1]
@@ -306,7 +306,7 @@
         (1,),
         [HELD] * (2 * parts),
         [HELD] * blocks,
-        [pltpu.VMEM((rows, width), F32)] + [pltpu.VMEM((rows, width), BF16)] * (blocks - 1),
+        [pltpu.VMEM((rows, width), F32 if keep and at == 0 else BF16) for at in range(blocks)],
         [],
         rows * blocks * width * 64,
         rows * blocks * width * 8,
@@ -611,18 +611,18 @@
     chunks = gather_rows(normed, chips)
     w, z = load_weights(weights, probe_signs)
     x = None
-    ps, gs, qs, ss, hids, tans, owns, gots = ([], [], [], [], [], [], [], [])
+    ps, gs, qs, ss, hids, tans, folded = ([], [], [], [], [], [], [])
     for at, blocks in enumerate(chunks):
         x, p, g, s, b, hid, own_q, sib_q = forward(
             blocks, w, at, len(chunks), x, quarter, BF16
         )
-        gots.append(to_sibling(sib_q, chips))
-        owns.append(own_q)
+        got = to_sibling(sib_q, chips)
+        folded += fold([own_q], [got], rows, at == 0)
         q, s, tan = tilt(z, at, x, p, g, s, b)
         for held, value in zip((ps, gs, qs, ss, hids, tans), (p, g, q, s, hid, tan)):
             held.append(value)
     own_t, sib_t = spread(w, z, tans, hids, BF16)
-    kept, *sent = fold(owns, gots, rows)
+    kept, *sent = folded
     kept = kept + offset
     for flip in range(1, chips):
         kept = kept + to_chip(sent[flip - 1], chips, flip).astype(F32)
@@ -637,7 +637,7 @@
     for at in range(probes):
         pieces.append(to_sibling(pieces[at], chips))
     got = to_sibling(sib_t, chips)
-    kept, *sent = fold([own_t], [got], rows)
+    kept, *sent = fold([own_t], [got], rows, True)
     for flip in range(1, chips):
         kept = kept + to_chip(sent[flip - 1], chips, flip).astype(F32)
     tan_dout = (kept / count).astype(BF16)

time: 187 us -> 178 us (0.952)
  local copies, waits for them, and re-layouts: 17.8 us -> 9.65 us
    unnamed x82 -> x50, local copies, waits for them, and re-layouts: 17.8 us -> 9.65 us
    pallas_call x11 -> x12, Pallas kernels: 52.1 us -> 52.2 us  [call(): pl.pallas_call(body, grid=grid, in_specs=in_specs, out_specs=out_specs, o...]
  transfers between devices with their start and end apart: 36 -> 36, of which waited for: 17 -> 15; matrix products, arithmetic and copies ran while one was open for 1% -> 1% of each run, Pallas kernels for 19% -> 19%
where the time goes in v2:
time: 178 us
  waiting for transfers between devices  67.7 us (38%)
  Pallas kernels  63.6 us (36%)
  starting transfers between devices  34.9 us (20%)
  local copies, waits for them, and re-layouts  9.65 us (5%)
    ppermute x15, waiting for transfers between devices, to_chip(): return lax.ppermute(x, 'mp', pairs)  58.4 us
    pallas_call x12, Pallas kernels, call(): pl.pallas_call(body, grid=grid, in_specs=in_specs, out_specs=out_specs, o...  52.2 us
    ppermute x15, starting transfers between devices, to_chip(): return lax.ppermute(x, 'mp', pairs)  24.6 us
    pallas_call x2, Pallas kernels, load(): pl.pallas_call(lambda *refs: load_kernel(plan, refs), name='load', in_spe...  11.4 us
    unnamed x50, local copies, waits for them, and re-layouts  9.65 us
    ppermute x6, starting transfers between devices, to_probe(): return lax.ppermute(x, 'probe', [(i, i ^ flip) for i in range(probes)])  8.05 us
    ppermute x6, waiting for transfers between devices, to_probe(): return lax.ppermute(x, 'probe', [(i, i ^ flip) for i in range(probes)])  7.15 us
  transfers between devices with their start and end apart: 36, of which 15 were waited for; matrix products, arithmetic and copies ran while one was open for 1% of the time, Pallas kernels for 19%

profile of v2, /device:TPU:0, one launch (start us, length us, event | category | flops | bytes accessed | tf_op | source)
XLA Modules:
  0.0 178.1 jit_solution(2474803392210806665)
XLA Ops:
  1.7 3.1 %collective-permute-start = (bf16[64,2048]{1,0:T(8,128)(2,1)S(1)}, bf16[64,2048]{1,0:T(8,128)(2,1)S(1)}, u32[]{:S(2)}, u32[]{:S(2)}) collective-permute-start(bf16[64,2048]{1,0:T(8,128)(2,1)S(1)} %shard_map.102.refs_0_), channel_id=1, source_target_pairs={{0,2},{1,3},{2,0},{3,1},{4,6},{5,7},{6,4},{7,5},{8,10},{9,11},{10,... | collective-permute-start | bytes 786440 | tf_op jit(solution)/shard_map/ppermute | solution.py:589
  4.9 2.5 %collective-permute-start.4 = (bf16[64,2048]{1,0:T(8,128)(2,1)S(1)}, bf16[64,2048]{1,0:T(8,128)(2,1)S(1)}, u32[]{:S(2)}, u32[]{:S(2)}) collective-permute-start(bf16[64,2048]{1,0:T(8,128)(2,1)S(1)} %shard_map.102.refs_0_), channel_id=1, source_target_pairs={{0,6},{1,7},{2,4},{3,5},{4,2},{5,3},{6,0},{7,1},{8,14},{9,15},{10,... | collective-permute-start | bytes 786440 | tf_op jit(solution)/shard_map/ppermute | solution.py:589
  7.5 4.1 %collective-permute-done.refs_1_ = bf16[64,2048]{1,0:T(8,128)(2,1)S(1)} collective-permute-done((bf16[64,2048]{1,0:T(8,128)(2,1)S(1)}, bf16[64,2048]{1,0:T(8,128)(2,1)S(1)}, u32[]{:S(2)}, u32[]{:S(2)}) %collective-permute-start) | collective-permute-done | bytes 262176 | tf_op jit(solution)/shard_map/ppermute | solution.py:589
  11.6 8.6 %collective-permute-done.4.refs_1_ = bf16[64,2048]{1,0:T(8,128)(2,1)S(1)} collective-permute-done((bf16[64,2048]{1,0:T(8,128)(2,1)S(1)}, bf16[64,2048]{1,0:T(8,128)(2,1)S(1)}, u32[]{:S(2)}, u32[]{:S(2)}) %collective-permute-start.4) | collective-permute-done | bytes 262176 | tf_op jit(solution)/shard_map/ppermute | solution.py:589
  20.2 10.1 %collective-permute-done.3.refs_0_ = bf16[64,2048]{1,0:T(8,128)(2,1)S(1)} collective-permute-done((bf16[64,2048]{1,0:T(8,128)(2,1)S(1)}, bf16[64,2048]{1,0:T(8,128)(2,1)S(1)}, u32[]{:S(2)}, u32[]{:S(2)}) %collective-permute-start.3) | collective-permute-done | bytes 262176 | tf_op jit(solution)/shard_map/ppermute | solution.py:589
  30.3 5.7 %load.2 = (bf16[6,320,2048]{2,1,0:T(8,128)(2,1)S(1)}, bf16[6,320,2048]{2,1,0:T(8,128)(2,1)S(1)}) custom-call(bf16[6,320,2048]{2,1,0:T(8,128)(2,1)} %bitcast.16, bf16[6,320,2048]{2,1,0:T(8,128)(2,1)} %bitcast.17), custom_call_target="tpu_custom_call" | custom-call | flops 503316480 | bytes 62914560 | tf_op jit(solution)/shard_map/load/pallas_call | solution.py:336
  36.1 3.5 %shard_map.103 = (bf16[512,2048]{1,0:T(8,128)(2,1)S(1)}, f32[640,256]{1,0:T(8,128)S(1)}, f32[640,256]{1,0:T(8,128)S(1)}, f32[640,256]{1,0:T(8,128)S(1)}, f32[640...) custom-call(bf16[64,2048]{1,0:T(8,128)(2,1)S(1)} %shard_map.102.refs_0_, ...), custom_call_target="tpu_custom_call" | custom-call | flops 1342177280 | bytes 12910592 | tf_op jit(solution)/shard_map/pallas_call | solution.py:86
  39.6 1.8 %shard_map.104 = (f32[640,256]{1,0:T(8,128)S(1)}, f32[640,256]{1,0:T(8,128)S(1)}, bf16[640,256]{1,0:T(8,128)(2,1)S(1)}) custom-call(bf16[3,640,2048]{2,1,0:T(8,128)(2,1)S(1)} %bitcast.12, bf16[512,2048]{1,0:T(8,128)(2,1)S(1)} %get-tuple-element.48.x.refs_5_, f32[640,256]{1,0:T(8,128)S(1)} %get-tuple-element.49.p.refs_12_.refs_14_, ...), custom_call_target="tpu_custom_call" | custom-call | flops 1342177280 | bytes 10551296 | tf_op jit(solution)/shard_map/pallas_call | solution.py:86
  42.2 3.5 %shard_map.105 = (bf16[512,2048]{1,0:T(8,128)(2,1)S(1)}, f32[640,256]{1,0:T(8,128)S(1)}, f32[640,256]{1,0:T(8,128)S(1)}, f32[640,256]{1,0:T(8,128)S(1)}, f32[640...) custom-call(bf16[64,2048]{1,0:T(8,128)(2,1)S(1)} %collective-permute, ...), custom_call_target="tpu_custom_call", output_to_operand_aliasing={{0}: (5, {})} | custom-call | flops 1342177280 | bytes 12910592 | tf_op jit(solution)/shard_map/pallas_call | solution.py:86
  45.8 1.8 %shard_map.106 = (f32[640,256]{1,0:T(8,128)S(1)}, f32[640,256]{1,0:T(8,128)S(1)}, bf16[640,256]{1,0:T(8,128)(2,1)S(1)}) custom-call(bf16[3,640,2048]{2,1,0:T(8,128)(2,1)S(1)} %bitcast.13, bf16[512,2048]{1,0:T(8,128)(2,1)S(1)} %get-tuple-element.54.x.refs_11_.refs_10_, f32[640,256]{1,0:T(8,128)S(1)} %get-tuple-element.55.p.refs_13_.refs_15_, ...), custom_call_target="tpu_custom_call" | custom-call | flops 1342177280 | bytes 10551296 | tf_op jit(solution)/shard_map/pallas_call | solution.py:86
  47.6 4.8 %shard_map.107 = (f32[256,2048]{1,0:T(8,128)S(1)}, bf16[256,2048]{1,0:T(8,128)(2,1)}) custom-call(bf16[3,640,2048]{2,1,0:T(8,128)(2,1)S(1)} %bitcast.11, bf16[3,640,2048]{2,1,0:T(8,128)(2,1)S(1)} %bitcast.14, bf16[640,256]{1,0:T(8,128)(2,1)S(1)} %get-tuple-element.53.refs_2_.refs_22_, bf16[640,256]{1,0:T(8,128)(2,1)S(1)} %get-tuple-element.59.refs_3_.refs_23_, ...), custom_call_target="tpu_custom_call" | custom-call | flops 2684354560 | bytes 8388608 | tf_op jit(solution)/shard_map/pallas_call | solution.py:86
  54.8 2.2 %collective-permute-done.18.refs_1_ = bf16[128,512]{1,0:T(8,128)(2,1)S(1)} collective-permute-done((bf16[128,512]{1,0:T(8,128)(2,1)S(1)}, bf16[128,512]{1,0:T(8,128)(2,1)S(1)}, u32[]{:S(2)}, u32[]{:S(2)}) %collective-permute-start.18) | collective-permute-done | bytes 131104 | tf_op jit(solution)/shard_map/ppermute | solution.py:584
  58.3 3.2 %collective-permute-start.21 = (bf16[64,512]{1,0:T(8,128)(2,1)}, bf16[64,512]{1,0:T(8,128)(2,1)}, u32[]{:S(2)}, u32[]{:S(2)}) collective-permute-start(bf16[64,512]{1,0:T(8,128)(2,1)} %get-tuple-element.74), channel_id=1, source_target_pairs={{0,4},{1,5},{2,6},{3,7},{4,0},{5,1},{6,2},{7,3},{8,12},{9,13},{10,... | collective-permute-start | bytes 196616 | tf_op jit(solution)/shard_map/ppermute | solution.py:589
  62.7 3.3 %collective-permute-done.21 = bf16[64,512]{1,0:T(8,128)(2,1)} collective-permute-done((bf16[64,512]{1,0:T(8,128)(2,1)}, bf16[64,512]{1,0:T(8,128)(2,1)}, u32[]{:S(2)}, u32[]{:S(2)}) %collective-permute-start.21) | collective-permute-done | bytes 65568 | tf_op jit(solution)/shard_map/ppermute | solution.py:589
  66.0 1.9 %collective-permute-done.22 = bf16[64,512]{1,0:T(8,128)(2,1)} collective-permute-done((bf16[64,512]{1,0:T(8,128)(2,1)}, bf16[64,512]{1,0:T(8,128)(2,1)}, u32[]{:S(2)}, u32[]{:S(2)}) %collective-permute-start.22) | collective-permute-done | bytes 65568 | tf_op jit(solution)/shard_map/ppermute | solution.py:589
  68.9 2.1 %collective-permute-start.25 = (bf16[64,512]{1,0:T(8,128)(2,1)S(1)}, bf16[64,512]{1,0:T(8,128)(2,1)S(1)}, u32[]{:S(2)}, u32[]{:S(2)}) collective-permute-start(bf16[64,512]{1,0:T(8,128)(2,1)S(1)} %multiply_convert_fusion.1), channel_id=1, source_target_pairs={{0,6},{1,7},{2,4},{3,5},{4,2},{5,3},{6,0},{7,1},{8,14},{9,15},{10,... | collective-permute-start | bytes 196616 | tf_op jit(solution)/shard_map/ppermute | solution.py:589
  71.5 1.9 %collective-permute-start.23 = (bf16[64,512]{1,0:T(8,128)(2,1)S(1)}, bf16[64,512]{1,0:T(8,128)(2,1)S(1)}, u32[]{:S(2)}, u32[]{:S(2)}) collective-permute-start(bf16[64,512]{1,0:T(8,128)(2,1)S(1)} %multiply_convert_fusion.1), channel_id=1, source_target_pairs={{0,2},{1,3},{2,0},{3,1},{4,6},{5,7},{6,4},{7,5},{8,10},{9,11},{10,... | collective-permute-start | bytes 196616 | tf_op jit(solution)/shard_map/ppermute | solution.py:589
  73.4 2.4 %collective-permute-done.25 = bf16[64,512]{1,0:T(8,128)(2,1)S(1)} collective-permute-done((bf16[64,512]{1,0:T(8,128)(2,1)S(1)}, bf16[64,512]{1,0:T(8,128)(2,1)S(1)}, u32[]{:S(2)}, u32[]{:S(2)}) %collective-permute-start.25) | collective-permute-done | bytes 65568 | tf_op jit(solution)/shard_map/ppermute | solution.py:589
  77.4 2.5 %collective-permute-start.28 = (bf16[256,512]{1,0:T(8,128)(2,1)S(1)}, bf16[256,512]{1,0:T(8,128)(2,1)S(1)}, u32[]{:S(2)}, u32[]{:S(2)}) collective-permute-start(bf16[256,512]{1,0:T(8,128)(2,1)S(1)} %pad_maximum_fusion.refs_0_), channel_id=1, source_target_pairs={{0,24},{8,16},{16,8},{24,0},{1,25},{9,17},{17,9},{25,1},{2,26},{10... | collective-permute-start | bytes 786440 | tf_op jit(solution)/shard_map/ppermute | solution.py:593
  83.7 2.5 %collective-permute-start.9 = (bf16[64,2048]{1,0:T(8,128)(2,1)S(1)}, bf16[64,2048]{1,0:T(8,128)(2,1)S(1)}, u32[]{:S(2)}, u32[]{:S(2)}) collective-permute-start(bf16[64,2048]{1,0:T(8,128)(2,1)S(1)} %get-tuple-element.66), channel_id=1, source_target_pairs={{0,4},{1,5},{2,6},{3,7},{4,0},{5,1},{6,2},{7,3},{8,12},{9,13},{10,... | collective-permute-start | bytes 786440 | tf_op jit(solution)/shard_map/ppermute | solution.py:589
  87.9 3.9 %collective-permute-done.27.refs_2_ = bf16[256,512]{1,0:T(8,128)(2,1)S(1)} collective-permute-done((bf16[256,512]{1,0:T(8,128)(2,1)S(1)}, bf16[256,512]{1,0:T(8,128)(2,1)S(1)}, u32[]{:S(2)}, u32[]{:S(2)}) %collective-permute-start.27) | collective-permute-done | bytes 262176 | tf_op jit(solution)/shard_map/ppermute | solution.py:593
  93.2 1.9 %collective-permute-done.8 = bf16[64,2048]{1,0:T(8,128)(2,1)S(1)} collective-permute-done((bf16[64,2048]{1,0:T(8,128)(2,1)S(1)}, bf16[64,2048]{1,0:T(8,128)(2,1)S(1)}, u32[]{:S(2)}, u32[]{:S(2)}) %collective-permute-start.8) | collective-permute-done | bytes 262176 | tf_op jit(solution)/shard_map/ppermute | solution.py:589
  95.1 9.9 %collective-permute-done.9 = bf16[64,2048]{1,0:T(8,128)(2,1)S(1)} collective-permute-done((bf16[64,2048]{1,0:T(8,128)(2,1)S(1)}, bf16[64,2048]{1,0:T(8,128)(2,1)S(1)}, u32[]{:S(2)}, u32[]{:S(2)}) %collective-permute-start.9) | collective-permute-done | bytes 262176 | tf_op jit(solution)/shard_map/ppermute | solution.py:589
  105.2 2.1 %collective-permute-start.15 = (bf16[64,2048]{1,0:T(8,128)(2,1)S(1)}, bf16[64,2048]{1,0:T(8,128)(2,1)S(1)}, u32[]{:S(2)}, u32[]{:S(2)}) collective-permute-start(bf16[64,2048]{1,0:T(8,128)(2,1)S(1)} %multiply_convert_fusion.refs_0_), channel_id=1, source_target_pairs={{0,6},{1,7},{2,4},{3,5},{4,2},{5,3},{6,0},{7,1},{8,14},{9,15},{10,... | collective-permute-start | bytes 786440 | tf_op jit(solution)/shard_map/ppermute | solution.py:589
  107.3 3.5 %collective-permute-start.14 = (bf16[64,2048]{1,0:T(8,128)(2,1)S(1)}, bf16[64,2048]{1,0:T(8,128)(2,1)S(1)}, u32[]{:S(2)}, u32[]{:S(2)}) collective-permute-start(bf16[64,2048]{1,0:T(8,128)(2,1)S(1)} %multiply_convert_fusion.refs_0_), channel_id=1, source_target_pairs={{0,4},{1,5},{2,6},{3,7},{4,0},{5,1},{6,2},{7,3},{8,12},{9,13},{10,... | collective-permute-start | bytes 786440 | tf_op jit(solution)/shard_map/ppermute | solution.py:589
  111.0 5.8 %load.3.refs_10_ = f32[12,160,2048]{2,1,0:T(8,128)S(1)} custom-call(f32[12,160,2048]{2,1,0:T(8,128)} %bitcast.18), custom_call_target="tpu_custom_call" | custom-call | flops 251658240 | bytes 31457280 | tf_op jit(solution)/shard_map/load/pallas_call | solution.py:336
  117.4 14.5 %collective-permute-done.14.refs_4_ = bf16[64,2048]{1,0:T(8,128)(2,1)S(1)} collective-permute-done((bf16[64,2048]{1,0:T(8,128)(2,1)S(1)}, bf16[64,2048]{1,0:T(8,128)(2,1)S(1)}, u32[]{:S(2)}, u32[]{:S(2)}) %collective-permute-start.14) | collective-permute-done | bytes 262176 | tf_op jit(solution)/shard_map/ppermute | solution.py:589
  132.4 15.3 %shard_map.111 = (f32[3,640,2048]{2,1,0:T(8,128)}, f32[12,160,2048]{2,1,0:T(8,128)S(1)}, f32[640,512]{1,0:T(8,128)S(1)}, f32[640,512]{1,0:T(8,128)S(1)}, f32[640,128]{1,0:T(8,128)S(1)}) custom-call(bf16[256,512]{1,0:T(8,128)(2,1)S(1)} %pad_maximum_fusion.refs_0_, ...), custom_call_target="tpu_custom_call", output_to_operand_aliasing={{1}: (10, {})} | custom-call | flops 8053063680 | bytes 45875200 | tf_op jit(solution)/shard_map/pallas_call | solution.py:86
  147.7 5.8 %copy-done = f32[12,160,2048]{2,1,0:T(8,128)} copy-done((f32[12,160,2048]{2,1,0:T(8,128)}, f32[12,160,2048]{2,1,0:T(8,128)S(1)}, u32[]{:S(2)}) %copy-start) | copy-done | bytes 15728664
  153.6 9.8 %shard_map.112.a = f32[48,320]{1,0:T(8,128)S(1)} custom-call(bf16[64,2048]{1,0:T(8,128)(2,1)S(1)} %multiply_convert_fusion.refs_0_, bf16[64,2048]{1,0:T(8,128)(2,1)S(1)} %collective-permute-done.11.refs_1_, bf16[64,2048]{1,0:T(8,128)(2,1)S(1)} %collective-permute-done.12.refs_2_, bf16[64,2048]{1,0:T(8,128)(2,1)S(1)} %collective-permute-done.13.refs_3_, ...), custom_call_target="tpu_custom_call" | custom-call | flops 5368709120 | bytes 16384000 | tf_op jit(solution)/shard_map/pallas_call | solution.py:86
  166.9 2.0 %collective-permute-done.35.d = f32[48,320]{1,0:T(8,128)S(1)} collective-permute-done((f32[48,320]{1,0:T(8,128)S(1)}, f32[48,320]{1,0:T(8,128)S(1)}, u32[]{:S(2)}, u32[]{:S(2)}) %collective-permute-start.35) | collective-permute-done | bytes 61472 | tf_op jit(solution)/shard_map/ppermute | solution.py:593
  170.2 8.0 %shard_map.113 = (f32[3,16,320]{2,1,0:T(8,128)}, f32[3,16,320]{2,1,0:T(8,128)}, f32[3,640,2048]{2,1,0:T(8,128)}) custom-call(f32[48,320]{1,0:T(8,128)S(1)} %shard_map.112.a, f32[48,320]{1,0:T(8,128)S(1)} %collective-permute-done.33.b, f32[48,320]{1,0:T(8,128)S(1)} %collective-permute-done.34.c, f32[48,320]{1,0:T(8,128)S(1)} %collective-permute-done.35.d, ...), custom_call_target="tpu_custom_call" | custom-call | flops 7864320 | bytes 31457280 | tf_op jit(solution)/shard_map/pallas_call | solution.py:86
  (107 shorter events, 23.3 us)
Async XLA Ops:
  1.7 9.8 %collective-permute-start = (bf16[64,2048]{1,0:T(8,128)(2,1)S(1)}, bf16[64,2048]{1,0:T(8,128)(2,1)S(1)}, u32[]{:S(2)}, u32[]{:S(2)}) collective-permute-start(bf16[64,2048]{1,0:T(8,128)(2,1)S(1)} %shard_map.102.refs_0_), channel_id=1, source_target_pairs={{0,2},{1,3},{2,0},{3,1},{4,6},{5,7},{6,4},{7,5},{8,10},{9,11},{10,... | collective-permute-start | bytes 786440 | tf_op jit(solution)/shard_map/ppermute | solution.py:589
  4.9 15.3 %collective-permute-start.4 = (bf16[64,2048]{1,0:T(8,128)(2,1)S(1)}, bf16[64,2048]{1,0:T(8,128)(2,1)S(1)}, u32[]{:S(2)}, u32[]{:S(2)}) collective-permute-start(bf16[64,2048]{1,0:T(8,128)(2,1)S(1)} %shard_map.102.refs_0_), channel_id=1, source_target_pairs={{0,6},{1,7},{2,4},{3,5},{4,2},{5,3},{6,0},{7,1},{8,14},{9,15},{10,... | collective-permute-start | bytes 786440 | tf_op jit(solution)/shard_map/ppermute | solution.py:589
  7.3 23.0 %collective-permute-start.3 = (bf16[64,2048]{1,0:T(8,128)(2,1)S(1)}, bf16[64,2048]{1,0:T(8,128)(2,1)S(1)}, u32[]{:S(2)}, u32[]{:S(2)}) collective-permute-start(bf16[64,2048]{1,0:T(8,128)(2,1)S(1)} %shard_map.102.refs_0_), channel_id=1, source_target_pairs={{0,4},{1,5},{2,6},{3,7},{4,0},{5,1},{6,2},{7,3},{8,12},{9,13},{10,... | collective-permute-start | bytes 786440 | tf_op jit(solution)/shard_map/ppermute | solution.py:589
  7.5 28.6 %collective-permute-start.1 = (bf16[64,2048]{1,0:T(8,128)(2,1)S(1)}, bf16[64,2048]{1,0:T(8,128)(2,1)S(1)}, u32[]{:S(2)}, u32[]{:S(2)}) collective-permute-start(bf16[64,2048]{1,0:T(8,128)(2,1)S(1)} %shard_map.102.refs_0_), channel_id=1, source_target_pairs={{0,1},{1,0},{2,3},{3,2},{4,5},{5,4},{6,7},{7,6},{8,9},{9,8},{10,11... | collective-permute-start | bytes 786440 | tf_op jit(solution)/shard_map/ppermute | solution.py:584
  11.6 24.5 %collective-permute-start.2 = (bf16[64,2048]{1,0:T(8,128)(2,1)S(1)}, bf16[64,2048]{1,0:T(8,128)(2,1)S(1)}, u32[]{:S(2)}, u32[]{:S(2)}) collective-permute-start(bf16[64,2048]{1,0:T(8,128)(2,1)S(1)} %collective-permute-done.refs_1_), channel_id=1, source_target_pairs={{0,1},{1,0},{2,3},{3,2},{4,5},{5,4},{6,7},{7,6},{8,9},{9,8},{10,11... | collective-permute-start | bytes 786440 | tf_op jit(solution)/shard_map/ppermute | solution.py:584
  20.2 22.0 %collective-permute-start.6 = (bf16[64,2048]{1,0:T(8,128)(2,1)S(1)}, bf16[64,2048]{1,0:T(8,128)(2,1)S(1)}, u32[]{:S(2)}, u32[]{:S(2)}) collective-permute-start(bf16[64,2048]{1,0:T(8,128)(2,1)S(1)} %collective-permute-done.4.refs_1_), channel_id=1, source_target_pairs={{0,1},{1,0},{2,3},{3,2},{4,5},{5,4},{6,7},{7,6},{8,9},{9,8},{10,11... | collective-permute-start | bytes 786440 | tf_op jit(solution)/shard_map/ppermute | solution.py:584
  30.3 11.9 %collective-permute-start.5 = (bf16[64,2048]{1,0:T(8,128)(2,1)S(1)}, bf16[64,2048]{1,0:T(8,128)(2,1)S(1)}, u32[]{:S(2)}, u32[]{:S(2)}) collective-permute-start(bf16[64,2048]{1,0:T(8,128)(2,1)S(1)} %collective-permute-done.3.refs_0_), channel_id=1, source_target_pairs={{0,1},{1,0},{2,3},{3,2},{4,5},{5,4},{6,7},{7,6},{8,9},{9,8},{10,11... | collective-permute-start | bytes 786440 | tf_op jit(solution)/shard_map/ppermute | solution.py:584
  53.8 26.6 %collective-permute-start.7 = (bf16[256,2048]{1,0:T(8,128)(2,1)}, bf16[256,2048]{1,0:T(8,128)(2,1)}, u32[]{:S(2)}, u32[]{:S(2)}) collective-permute-start(bf16[256,2048]{1,0:T(8,128)(2,1)} %get-tuple-element.63), channel_id=1, source_target_pairs={{0,1},{1,0},{2,3},{3,2},{4,5},{5,4},{6,7},{7,6},{8,9},{9,8},{10,11... | collective-permute-start | bytes 3145736 | tf_op jit(solution)/shard_map/ppermute | solution.py:584
  58.3 7.7 %collective-permute-start.21 = (bf16[64,512]{1,0:T(8,128)(2,1)}, bf16[64,512]{1,0:T(8,128)(2,1)}, u32[]{:S(2)}, u32[]{:S(2)}) collective-permute-start(bf16[64,512]{1,0:T(8,128)(2,1)} %get-tuple-element.74), channel_id=1, source_target_pairs={{0,4},{1,5},{2,6},{3,7},{4,0},{5,1},{6,2},{7,3},{8,12},{9,13},{10,... | collective-permute-start | bytes 196616 | tf_op jit(solution)/shard_map/ppermute | solution.py:589
  61.5 6.4 %collective-permute-start.22 = (bf16[64,512]{1,0:T(8,128)(2,1)}, bf16[64,512]{1,0:T(8,128)(2,1)}, u32[]{:S(2)}, u32[]{:S(2)}) collective-permute-start(bf16[64,512]{1,0:T(8,128)(2,1)} %get-tuple-element.75), channel_id=1, source_target_pairs={{0,6},{1,7},{2,4},{3,5},{4,2},{5,3},{6,0},{7,1},{8,14},{9,15},{10,... | collective-permute-start | bytes 196616 | tf_op jit(solution)/shard_map/ppermute | solution.py:589
  68.9 6.8 %collective-permute-start.25 = (bf16[64,512]{1,0:T(8,128)(2,1)S(1)}, bf16[64,512]{1,0:T(8,128)(2,1)S(1)}, u32[]{:S(2)}, u32[]{:S(2)}) collective-permute-start(bf16[64,512]{1,0:T(8,128)(2,1)S(1)} %multiply_convert_fusion.1), channel_id=1, source_target_pairs={{0,6},{1,7},{2,4},{3,5},{4,2},{5,3},{6,0},{7,1},{8,14},{9,15},{10,... | collective-permute-start | bytes 196616 | tf_op jit(solution)/shard_map/ppermute | solution.py:589
  71.0 6.4 %collective-permute-start.24 = (bf16[64,512]{1,0:T(8,128)(2,1)S(1)}, bf16[64,512]{1,0:T(8,128)(2,1)S(1)}, u32[]{:S(2)}, u32[]{:S(2)}) collective-permute-start(bf16[64,512]{1,0:T(8,128)(2,1)S(1)} %multiply_convert_fusion.1), channel_id=1, source_target_pairs={{0,4},{1,5},{2,6},{3,7},{4,0},{5,1},{6,2},{7,3},{8,12},{9,13},{10,... | collective-permute-start | bytes 196616 | tf_op jit(solution)/shard_map/ppermute | solution.py:589
  71.5 5.9 %collective-permute-start.23 = (bf16[64,512]{1,0:T(8,128)(2,1)S(1)}, bf16[64,512]{1,0:T(8,128)(2,1)S(1)}, u32[]{:S(2)}, u32[]{:S(2)}) collective-permute-start(bf16[64,512]{1,0:T(8,128)(2,1)S(1)} %multiply_convert_fusion.1), channel_id=1, source_target_pairs={{0,2},{1,3},{2,0},{3,1},{4,6},{5,7},{6,4},{7,5},{8,10},{9,11},{10,... | collective-permute-start | bytes 196616 | tf_op jit(solution)/shard_map/ppermute | solution.py:589
  77.4 10.5 %collective-permute-start.28 = (bf16[256,512]{1,0:T(8,128)(2,1)S(1)}, bf16[256,512]{1,0:T(8,128)(2,1)S(1)}, u32[]{:S(2)}, u32[]{:S(2)}) collective-permute-start(bf16[256,512]{1,0:T(8,128)(2,1)S(1)} %pad_maximum_fusion.refs_0_), channel_id=1, source_target_pairs={{0,24},{8,16},{16,8},{24,0},{1,25},{9,17},{17,9},{25,1},{2,26},{10... | collective-permute-start | bytes 786440 | tf_op jit(solution)/shard_map/ppermute | solution.py:593
  79.9 11.8 %collective-permute-start.27 = (bf16[256,512]{1,0:T(8,128)(2,1)S(1)}, bf16[256,512]{1,0:T(8,128)(2,1)S(1)}, u32[]{:S(2)}, u32[]{:S(2)}) collective-permute-start(bf16[256,512]{1,0:T(8,128)(2,1)S(1)} %pad_maximum_fusion.refs_0_), channel_id=1, source_target_pairs={{0,16},{8,24},{16,0},{24,8},{1,17},{9,25},{17,1},{25,9},{2,18},{10... | collective-permute-start | bytes 786440 | tf_op jit(solution)/shard_map/ppermute | solution.py:593
  83.4 11.7 %collective-permute-start.8 = (bf16[64,2048]{1,0:T(8,128)(2,1)S(1)}, bf16[64,2048]{1,0:T(8,128)(2,1)S(1)}, u32[]{:S(2)}, u32[]{:S(2)}) collective-permute-start(bf16[64,2048]{1,0:T(8,128)(2,1)S(1)} %get-tuple-element.65), channel_id=1, source_target_pairs={{0,2},{1,3},{2,0},{3,1},{4,6},{5,7},{6,4},{7,5},{8,10},{9,11},{10,... | collective-permute-start | bytes 786440 | tf_op jit(solution)/shard_map/ppermute | solution.py:589
  83.7 21.3 %collective-permute-start.9 = (bf16[64,2048]{1,0:T(8,128)(2,1)S(1)}, bf16[64,2048]{1,0:T(8,128)(2,1)S(1)}, u32[]{:S(2)}, u32[]{:S(2)}) collective-permute-start(bf16[64,2048]{1,0:T(8,128)(2,1)S(1)} %get-tuple-element.66), channel_id=1, source_target_pairs={{0,4},{1,5},{2,6},{3,7},{4,0},{5,1},{6,2},{7,3},{8,12},{9,13},{10,... | collective-permute-start | bytes 786440 | tf_op jit(solution)/shard_map/ppermute | solution.py:589
  86.2 18.8 %collective-permute-start.10 = (bf16[64,2048]{1,0:T(8,128)(2,1)S(1)}, bf16[64,2048]{1,0:T(8,128)(2,1)S(1)}, u32[]{:S(2)}, u32[]{:S(2)}) collective-permute-start(bf16[64,2048]{1,0:T(8,128)(2,1)S(1)} %get-tuple-element.67), channel_id=1, source_target_pairs={{0,6},{1,7},{2,4},{3,5},{4,2},{5,3},{6,0},{7,1},{8,14},{9,15},{10,... | collective-permute-start | bytes 786440 | tf_op jit(solution)/shard_map/ppermute | solution.py:589
  87.9 19.4 %collective-permute-start.29 = (bf16[256,512]{1,0:T(8,128)(2,1)S(1)}, bf16[256,512]{1,0:T(8,128)(2,1)S(1)}, u32[]{:S(2)}, u32[]{:S(2)}) collective-permute-start(bf16[256,512]{1,0:T(8,128)(2,1)S(1)} %pad_maximum_fusion.refs_0_), channel_id=1, source_target_pairs={{0,1},{1,0},{2,3},{3,2},{4,5},{5,4},{6,7},{7,6},{8,9},{9,8},{10,11... | collective-permute-start | bytes 786440 | tf_op jit(solution)/shard_map/ppermute | solution.py:584
  91.7 19.0 %collective-permute-start.26 = (bf16[256,512]{1,0:T(8,128)(2,1)S(1)}, bf16[256,512]{1,0:T(8,128)(2,1)S(1)}, u32[]{:S(2)}, u32[]{:S(2)}) collective-permute-start(bf16[256,512]{1,0:T(8,128)(2,1)S(1)} %pad_maximum_fusion.refs_0_), channel_id=1, source_target_pairs={{0,8},{8,0},{16,24},{24,16},{1,9},{9,1},{17,25},{25,17},{2,10},{10... | collective-permute-start | bytes 786440 | tf_op jit(solution)/shard_map/ppermute | solution.py:593
  95.1 15.7 %collective-permute-start.32 = (bf16[256,512]{1,0:T(8,128)(2,1)S(1)}, bf16[256,512]{1,0:T(8,128)(2,1)S(1)}, u32[]{:S(2)}, u32[]{:S(2)}) collective-permute-start(bf16[256,512]{1,0:T(8,128)(2,1)S(1)} %collective-permute-done.28.refs_3_), channel_id=1, source_target_pairs={{0,1},{1,0},{2,3},{3,2},{4,5},{5,4},{6,7},{7,6},{8,9},{9,8},{10,11... | collective-permute-start | bytes 786440 | tf_op jit(solution)/shard_map/ppermute | solution.py:584
  105.0 11.7 %collective-permute-start.31 = (bf16[256,512]{1,0:T(8,128)(2,1)S(1)}, bf16[256,512]{1,0:T(8,128)(2,1)S(1)}, u32[]{:S(2)}, u32[]{:S(2)}) collective-permute-start(bf16[256,512]{1,0:T(8,128)(2,1)S(1)} %collective-permute-done.27.refs_2_), channel_id=1, source_target_pairs={{0,1},{1,0},{2,3},{3,2},{4,5},{5,4},{6,7},{7,6},{8,9},{9,8},{10,11... | collective-permute-start | bytes 786440 | tf_op jit(solution)/shard_map/ppermute | solution.py:584
  105.2 12.1 %collective-permute-start.15 = (bf16[64,2048]{1,0:T(8,128)(2,1)S(1)}, bf16[64,2048]{1,0:T(8,128)(2,1)S(1)}, u32[]{:S(2)}, u32[]{:S(2)}) collective-permute-start(bf16[64,2048]{1,0:T(8,128)(2,1)S(1)} %multiply_convert_fusion.refs_0_), channel_id=1, source_target_pairs={{0,6},{1,7},{2,4},{3,5},{4,2},{5,3},{6,0},{7,1},{8,14},{9,15},{10,... | collective-permute-start | bytes 786440 | tf_op jit(solution)/shard_map/ppermute | solution.py:589
  107.3 24.6 %collective-permute-start.14 = (bf16[64,2048]{1,0:T(8,128)(2,1)S(1)}, bf16[64,2048]{1,0:T(8,128)(2,1)S(1)}, u32[]{:S(2)}, u32[]{:S(2)}) collective-permute-start(bf16[64,2048]{1,0:T(8,128)(2,1)S(1)} %multiply_convert_fusion.refs_0_), channel_id=1, source_target_pairs={{0,4},{1,5},{2,6},{3,7},{4,0},{5,1},{6,2},{7,3},{8,12},{9,13},{10,... | collective-permute-start | bytes 786440 | tf_op jit(solution)/shard_map/ppermute | solution.py:589
  110.8 21.1 %collective-permute-start.11 = (bf16[64,2048]{1,0:T(8,128)(2,1)S(1)}, bf16[64,2048]{1,0:T(8,128)(2,1)S(1)}, u32[]{:S(2)}, u32[]{:S(2)}) collective-permute-start(bf16[64,2048]{1,0:T(8,128)(2,1)S(1)} %multiply_convert_fusion.refs_0_), channel_id=1, source_target_pairs={{0,2},{1,3},{2,0},{3,1},{4,6},{5,7},{6,4},{7,5},{8,10},{9,11},{10,... | collective-permute-start | bytes 786440 | tf_op jit(solution)/shard_map/ppermute | solution.py:589
  110.8 21.6 %collective-permute-start.30 = (bf16[256,512]{1,0:T(8,128)(2,1)S(1)}, bf16[256,512]{1,0:T(8,128)(2,1)S(1)}, u32[]{:S(2)}, u32[]{:S(2)}) collective-permute-start(bf16[256,512]{1,0:T(8,128)(2,1)S(1)} %collective-permute-done.26.refs_1_), channel_id=1, source_target_pairs={{0,1},{1,0},{2,3},{3,2},{4,5},{5,4},{6,7},{7,6},{8,9},{9,8},{10,11... | collective-permute-start | bytes 786440 | tf_op jit(solution)/shard_map/ppermute | solution.py:584
  116.7 36.8 %collective-permute-start.12 = (bf16[64,2048]{1,0:T(8,128)(2,1)S(1)}, bf16[64,2048]{1,0:T(8,128)(2,1)S(1)}, u32[]{:S(2)}, u32[]{:S(2)}) collective-permute-start(bf16[64,2048]{1,0:T(8,128)(2,1)S(1)} %multiply_convert_fusion.refs_0_), channel_id=1, source_target_pairs={{0,1},{1,0},{2,3},{3,2},{4,5},{5,4},{6,7},{7,6},{8,9},{9,8},{10,11... | collective-permute-start | bytes 786440 | tf_op jit(solution)/shard_map/ppermute | solution.py:584
  117.3 36.2 %collective-permute-start.17 = (bf16[64,2048]{1,0:T(8,128)(2,1)S(1)}, bf16[64,2048]{1,0:T(8,128)(2,1)S(1)}, u32[]{:S(2)}, u32[]{:S(2)}) collective-permute-start(bf16[64,2048]{1,0:T(8,128)(2,1)S(1)} %collective-permute-done.15.refs_5_), channel_id=1, source_target_pairs={{0,1},{1,0},{2,3},{3,2},{4,5},{5,4},{6,7},{7,6},{8,9},{9,8},{10,11... | collective-permute-start | bytes 786440 | tf_op jit(solution)/shard_map/ppermute | solution.py:584
  131.8 21.7 %collective-permute-start.16 = (bf16[64,2048]{1,0:T(8,128)(2,1)S(1)}, bf16[64,2048]{1,0:T(8,128)(2,1)S(1)}, u32[]{:S(2)}, u32[]{:S(2)}) collective-permute-start(bf16[64,2048]{1,0:T(8,128)(2,1)S(1)} %collective-permute-done.14.refs_4_), channel_id=1, source_target_pairs={{0,1},{1,0},{2,3},{3,2},{4,5},{5,4},{6,7},{7,6},{8,9},{9,8},{10,11... | collective-permute-start | bytes 786440 | tf_op jit(solution)/shard_map/ppermute | solution.py:584
  131.8 21.7 %collective-permute-start.13 = (bf16[64,2048]{1,0:T(8,128)(2,1)S(1)}, bf16[64,2048]{1,0:T(8,128)(2,1)S(1)}, u32[]{:S(2)}, u32[]{:S(2)}) collective-permute-start(bf16[64,2048]{1,0:T(8,128)(2,1)S(1)} %collective-permute-done.11.refs_1_), channel_id=1, source_target_pairs={{0,1},{1,0},{2,3},{3,2},{4,5},{5,4},{6,7},{7,6},{8,9},{9,8},{10,11... | collective-permute-start | bytes 786440 | tf_op jit(solution)/shard_map/ppermute | solution.py:584
  163.3 5.5 %collective-permute-start.35 = (f32[48,320]{1,0:T(8,128)S(1)}, f32[48,320]{1,0:T(8,128)S(1)}, u32[]{:S(2)}, u32[]{:S(2)}) collective-permute-start(f32[48,320]{1,0:T(8,128)S(1)} %shard_map.112.a), channel_id=1, source_target_pairs={{0,24},{8,16},{16,8},{24,0},{1,25},{9,17},{17,9},{25,1},{2,26},{10... | collective-permute-start | bytes 184328 | tf_op jit(solution)/shard_map/ppermute | solution.py:593
  164.9 5.2 %collective-permute-start.34 = (f32[48,320]{1,0:T(8,128)S(1)}, f32[48,320]{1,0:T(8,128)S(1)}, u32[]{:S(2)}, u32[]{:S(2)}) collective-permute-start(f32[48,320]{1,0:T(8,128)S(1)} %shard_map.112.a), channel_id=1, source_target_pairs={{0,16},{8,24},{16,0},{24,8},{1,17},{9,25},{17,1},{25,9},{2,18},{10... | collective-permute-start | bytes 184328 | tf_op jit(solution)/shard_map/ppermute | solution.py:593
  (29 other events, 325.0 us)
